TPU v7x, 32 devices: a whole 2x2x4 slice. The times are simulated.
32 devices in a mesh: expert: 4 (over y, x), shard: 8 (over z, core).
Axes of the slice: x: 2, y: 2, z: 4, core: 2. Of those that a mesh axis runs over, the one named last changes fastest.
Arguments:
- tokens: bfloat16 [256, 6144], P(('expert', 'shard')), may hold values from -6 to 6
- norm_gain: float32 [6144], replicated, may hold values from 0.5 to 1.5
- routes: int32 [256, 2], P(('expert', 'shard')), may hold values from 0 to 3, all different within a row; in each aligned block of 8 rows (0 to 7, 8 to 15, ...) at most 4 rows name the same one
- gate_weights: float32 [256, 2], P(('expert', 'shard')), may hold values from 0.2 to 1
- capacity: int32 [4], replicated, may hold values from 2 to 4
- w_gate: bfloat16 [4, 6144, 8192], P('expert', None, 'shard'), may hold values from -0.078125 to 0.078125
- w_up: bfloat16 [4, 6144, 8192], P('expert', None, 'shard'), may hold values from -0.078125 to 0.078125
- w_down: bfloat16 [4, 8192, 6144], P('expert', 'shard'), may hold values from -0.0625 to 0.0625
Outputs:
- mixed_out: bfloat16 [256, 6144], P(('expert', 'shard'))
Inputs may be any that keep to these rules, and one draw needn't show every extreme that they name: `routes`: each row names 2 different experts; among the rows of one device no expert is named by more than 4 rows.
All inputs are finite; a program needn't handle non-finite values.
Results may differ from a plain program's by a relative error of at most 0.019.
Values may be sent and summed in bfloat16 or wider, within the bound.
No kernel may reach another device: no remote copies, remote signals or barrier semaphores. Data moves between devices by JAX's collectives and lax.ppermute only.
A program may use at most 128 MiB of HBM per device.

v0:
```python
import jax
import jax.numpy as jnp
from jax import lax
from jax.sharding import Mesh, PartitionSpec as P
import jax.experimental.pallas as pl
import jax.experimental.pallas.tpu as pltpu

CORES = 2
MIB = 1 << 20
LANES = 128
MOST_VMEM = 67035136
PARTS_IN = 1
CUTS = (6,)
TILE = 256
MIX_PARTS = 6
VMEM = pltpu.VMEM
SMEM = pltpu.SMEM


def whole(space=VMEM):
    return pl.BlockSpec(memory_space=space)


def params(mib):
    return pltpu.CompilerParams(vmem_limit_bytes=mib * MIB)


def home_kernel(depth, cap_hbm, tok_hbm, gain_hbm, routes_hbm, gates_hbm, *refs):
    meta_ref, cap_ref, tok_ref, gain_ref, routes_ref, gates_ref, sem = refs[-7:]
    exts = refs[:-7]
    small = [(cap_hbm, cap_ref), (routes_hbm, routes_ref), (gates_hbm, gates_ref)]
    pairs = small + [(tok_hbm, tok_ref), (gain_hbm, gain_ref)]
    copies = [pltpu.make_async_copy(src, dst, sem.at[i]) for i, (src, dst) in enumerate(pairs)]
    for c in copies:
        c.start()
    tok, width = tok_ref.shape
    row = lax.broadcasted_iota(jnp.int32, (tok, tok), 0)
    col = lax.broadcasted_iota(jnp.int32, (tok, tok), 1)
    for c in copies[:3]:
        c.wait()

    def upright(line):
        return jnp.sum(jnp.where(row == col, line, 0.0), axis=1, keepdims=True)

    across = routes_ref[...].astype(jnp.float32)
    codes = []
    for k in range(2):
        mine = upright(across[k:k + 1, :])
        same = (across[0:1, :] == mine) | (across[1:2, :] == mine)
        rank = jnp.sum(jnp.where(same & (col < row), 1.0, 0.0), axis=1, keepdims=True)
        cap = jnp.zeros_like(mine)
        for e in range(cap_ref.shape[0]):
            cap = jnp.where(mine == e, cap_ref[e].astype(jnp.float32), cap)
        codes.append(jnp.where(rank < cap, mine * depth + rank, -1.0))
    lane = lax.broadcasted_iota(jnp.int32, (tok, LANES), 1)
    code = jnp.where(lane == 0, codes[0], jnp.where(lane == 1, codes[1], 0.0))
    gate = [upright(gates_ref[k:k + 1, :]) for k in range(2)]
    meta_ref[...] = code + jnp.where(lane == 2, gate[0], jnp.where(lane == 3, gate[1], 0.0))
    step = width // len(exts)
    exts[0][:, step:] = code.astype(jnp.bfloat16)
    for c in copies[3:]:
        c.wait()
    wide = tok_ref[...].astype(jnp.float32)
    scale = lax.rsqrt(jnp.mean(wide * wide, axis=-1, keepdims=True) + 1e-05)
    normed = (wide * scale * gain_ref[...]).astype(jnp.bfloat16)
    for i, ext_ref in enumerate(exts):
        ext_ref[:, :step] = normed[:, i * step:(i + 1) * step]


def pack_kernel(depth, zs, first, *refs):
    sources = zs if first else 2 * zs
    experts = len(refs) - sources
    me = lax.axis_index("expert")
    ins, data, outs = refs[:zs], refs[sources - zs:sources], refs[sources:]
    tok = ins[0].shape[0]
    width = outs[0].shape[1]
    rows = experts * zs * depth
    picks = []
    row = lax.broadcasted_iota(jnp.int32, (tok, rows), 1)
    k, o, slot = row // (zs * depth), (row // depth) % zs, row % depth
    target = slot
    for i in range(experts):
        target = jnp.where(k == i, slot + (me ^ i) * depth, target)
    target = target.astype(jnp.float32)
    for i in range(zs):
        code = ins[i][:, ins[i].shape[1] - LANES:].astype(jnp.float32)
        hit = (code[:, 0:1] == target) | (code[:, 1:2] == target)
        picks.append(jnp.where(hit & (o == i), 1.0, 0.0))
    pick = jnp.concatenate(picks, axis=0).T.astype(jnp.bfloat16)
    normed = jnp.concatenate([r[:, :width].astype(jnp.float32) for r in data], axis=0).astype(jnp.bfloat16)
    packed = jnp.dot(pick, normed, preferred_element_type=jnp.float32).astype(jnp.bfloat16)
    step = zs * depth
    for i in range(experts):
        outs[i][...] = packed[i * step:(i + 1) * step]


def up_kernel(zs, depth, part, parts, *refs):
    experts = lax.axis_size("expert")
    blocks, (gate_ref, up_ref), refs = refs[:CORES * experts], refs[CORES * experts:CORES * experts + 2], refs[CORES * experts + 2:]
    before = ()
    if part:
        before, refs = refs[:2], refs[2:]
    step, width = blocks[0].shape
    outs = refs[:-1] if part < parts - 1 else refs[:-2]
    x_ref = refs[len(outs)]
    rows = x_ref.shape[0]
    for i, r in enumerate(blocks):
        x_ref[i * step:(i + 1) * step, :] = r[...]
    tile = 256
    span = slice(part * width, (part + 1) * width)
    for n in range(gate_ref.shape[1] // tile):
        cols = slice(n * tile, (n + 1) * tile)
        g = jnp.dot(x_ref[...], gate_ref[span, cols], preferred_element_type=jnp.float32)
        u = jnp.dot(x_ref[...], up_ref[span, cols], preferred_element_type=jnp.float32)
        if part:
            g = g + before[0][:, cols]
            u = u + before[1][:, cols]
        if part < parts - 1:
            outs[0][:, cols] = g
            outs[1][:, cols] = u
        else:
            refs[-1][:, cols] = (g / (1.0 + jnp.exp(-g)) * u).astype(jnp.bfloat16)
    if part < parts - 1:
        return
    hid_ref, h_ref = outs[0], refs[-1]
    chip, me = lax.axis_index("chip"), lax.axis_index("expert")
    row = lax.broadcasted_iota(jnp.int32, (rows, rows), 0)
    col = lax.broadcasted_iota(jnp.int32, (rows, rows), 1)
    slot, z = row % depth, (row // depth) % zs
    e, side = (row // (depth * zs)) % experts, row // (depth * zs * experts)
    block = jnp.zeros_like(e)
    for i in range(experts):
        block = jnp.where(e == (me ^ i), i, block)
    source = ((side * experts + block) * zs + (z ^ chip)) * depth + slot
    order = jnp.where(source == col, 1.0, 0.0).astype(jnp.bfloat16)
    hid_ref[...] = jnp.dot(order, h_ref[...], preferred_element_type=jnp.float32).astype(jnp.bfloat16)


def down_kernel(start, hid_ref, down_ref, kept_ref, sent_ref):
    mine, span = kept_ref.shape
    for n in range(span // TILE):
        cols = slice(start + n * TILE, start + (n + 1) * TILE)
        d = jnp.dot(hid_ref[...], down_ref[:, cols], preferred_element_type=jnp.float32)
        kept_ref[:, n * TILE:(n + 1) * TILE] = d[:mine]
        sent_ref[:, n * TILE:(n + 1) * TILE] = d[mine:].astype(jnp.bfloat16)


def join_kernel(*refs):
    out_ref = refs[-1]
    blocks, depth, width = out_ref.shape
    start = 0
    for kept_ref, sent_ref in zip(refs[:-1:2], refs[1:-1:2]):
        cols = slice(start, start + kept_ref.shape[1])
        both = kept_ref[...] + sent_ref[...].astype(jnp.float32)
        for b in range(blocks):
            out_ref[b, :, cols] = both[b * depth:(b + 1) * depth].astype(jnp.bfloat16)
        start = cols.stop


def mix_kernel(meta_ref, parts_ref, out_ref):
    experts, zs, depth, width = parts_ref.shape
    meta = meta_ref[...]
    weights = []
    for target in range(experts * depth):
        w = jnp.where(meta[:, 1:2] == target, meta[:, 3:4], 0.0)
        weights.append(jnp.where(meta[:, 0:1] == target, meta[:, 2:3], w))
    step = width // MIX_PARTS
    for c in range(MIX_PARTS):
        cols = slice(c * step, (c + 1) * step)
        mixed = jnp.zeros((out_ref.shape[0], step), jnp.float32)
        for e in range(experts):
            total = parts_ref[e, 0, :, cols].astype(jnp.float32)
            for z in range(1, zs):
                total = total + parts_ref[e, z, :, cols].astype(jnp.float32)
            total = total.astype(jnp.bfloat16).astype(jnp.float32)
            for k in range(depth):
                mixed = mixed + weights[e * depth + k] * total[k:k + 1, :]
        out_ref[:, cols] = mixed.astype(jnp.bfloat16)


def flips(count):
    masks = [count - 1] if count > 1 else []
    bit = 1
    while 2 * bit < count:
        masks.append(bit)
        bit *= 2
    if bit * 2 != count and count > 1:
        raise ValueError("axis size")
    return masks


def flip(value, axis, mask):
    return lax.ppermute(value, axis, [(i, i ^ mask) for i in range(lax.axis_size(axis))])


def on_device(tokens, norm_gain, routes, gate_weights, capacity, w_gate, w_up, w_down):
    experts, zs = lax.axis_size("expert"), lax.axis_size("chip")
    tok, width = tokens.shape
    hidden = w_gate.shape[2]
    depth = max(tok // 2, tok * routes.shape[1] // capacity.shape[0])
    swap = lambda v: flip(v, "core", 1)
    rows = CORES * experts * zs * depth
    f32, bf16 = jnp.float32, jnp.bfloat16
    scope = jax.named_scope

    part = width // PARTS_IN
    sizes = [part + LANES] + [part] * (PARTS_IN - 1)
    *exts, meta = pl.pallas_call(
        lambda *r: home_kernel(depth, *r),
        out_shape=[VMEM((tok, n), bf16) for n in sizes] + [VMEM((tok, LANES), f32)],
        in_specs=[whole(pl.ANY)] * 5,
        out_specs=[whole()] * (PARTS_IN + 1),
        scratch_shapes=[
            SMEM(capacity.shape, jnp.int32),
            VMEM((tok, width), bf16),
            VMEM((1, width), f32),
            VMEM((2, tok), jnp.int32),
            VMEM((2, tok), f32),
            pltpu.SemaphoreType.DMA((5,)),
        ],
        compiler_params=pltpu.CompilerParams(vmem_limit_bytes=MOST_VMEM - tok * (2 * (width + LANES) + 4 * LANES)),
        name="home",
    )(capacity, tokens, norm_gain.reshape(1, width), routes.T, gate_weights.T)

    gathered = []
    for i in range(PARTS_IN):
        near = {0: exts[i]}
        for mask in flips(zs):
            for o in list(near):
                near[o ^ mask] = flip(near[o], "chip", mask)
        gathered.append([near[o] for o in range(zs)])
    acc = ()
    for i in range(PARTS_IN):
        first = i == 0
        sources = gathered[0] + ([] if first else gathered[i])
        packed = pl.pallas_call(
            lambda *r, first=first: pack_kernel(depth, zs, first, *r),
            out_shape=[jax.ShapeDtypeStruct((zs * depth, part), bf16)] * experts,
            in_specs=[whole()] * len(sources),
            out_specs=[whole()] * experts,
            compiler_params=params(8),
            cost_estimate=pl.CostEstimate(flops=10**11 if first else 10**6, bytes_accessed=0, transcendentals=0),
            name=f"pack_{i}",
        )(*sources)
        arrived = [packed[0]] + [flip(packed[k], "expert", k) for k in range(1, experts)]
        theirs = [swap(v) for v in arrived]
        last = i == PARTS_IN - 1
        total = jax.ShapeDtypeStruct((rows, hidden), f32)
        scratch = [VMEM((rows, part), bf16)] + ([VMEM((rows, hidden), bf16)] if last else [])
        acc = pl.pallas_call(
            lambda *r, i=i: up_kernel(zs, depth, i, PARTS_IN, *r),
            out_shape=[jax.ShapeDtypeStruct((rows, hidden), bf16)] if last else [total, total],
            in_specs=[whole()] * (CORES * experts + 2 + len(acc)),
            out_specs=[whole()] * (1 if last else 2),
            scratch_shapes=scratch,
            compiler_params=params(10 if rows <= 128 else 22),
            name=f"up_{i}",
        )(*arrived, *theirs, w_gate[0], w_up[0], *acc)
    hid = acc[0]
    mine = rows // CORES
    tiles = width // TILE
    bounds = [0, *[tiles * k // 8 * TILE for k in CUTS], width]
    halves = []
    for j, (start, stop) in enumerate(zip(bounds[:-1], bounds[1:])):
        kept, sent = pl.pallas_call(
            lambda *r, start=start: down_kernel(start, *r),
            out_shape=[jax.ShapeDtypeStruct((mine, stop - start), dtype) for dtype in (f32, bf16)],
            in_specs=[whole(), whole()],
            out_specs=[whole()] * 2,
            compiler_params=params(8),
            cost_estimate=pl.CostEstimate(flops=4 * mine * (stop - start) * hidden, bytes_accessed=0, transcendentals=0),
            name=f"down_{j}",
        )(hid, w_down[0])
        halves += [kept, swap(sent)]
    partial = pl.pallas_call(
        join_kernel,
        out_shape=jax.ShapeDtypeStruct((experts * zs, depth, width), bf16),
        in_specs=[whole()] * len(halves),
        out_specs=whole(),
        compiler_params=params(4 if mine <= 64 else 30),
        name="join",
    )(*halves)
    pieces = lax.all_to_all(partial, ("expert", "chip"), split_axis=0, concat_axis=0, tiled=True)
    return pl.pallas_call(
        mix_kernel,
        out_shape=jax.ShapeDtypeStruct((tok, width), bf16),
        in_specs=[whole()] * 2,
        out_specs=whole(),
        compiler_params=params(16),
        name="mix",
    )(meta, pieces.reshape(experts, zs, depth, width))


def solution(mesh):
    experts, shards = mesh.shape["expert"], mesh.shape["shard"]
    devices = mesh.devices.reshape(experts, shards // CORES, CORES)
    split = Mesh(devices, ("expert", "chip", "core"))
    everywhere = P(("expert", "chip", "core"), None)
    columns = P("expert", None, ("chip", "core"))
    in_specs = (
        everywhere, P(), everywhere, everywhere, P(),
        columns, columns, P("expert", ("chip", "core"), None),
    )
    step = jax.shard_map(on_device, mesh=split, in_specs=in_specs, out_specs=everywhere, check_vma=False)
    return step
```

profile of v0, /device:TPU:0, one launch (start us, length us, event | category | flops | bytes accessed | tf_op | source)
XLA Modules:
  0.0 64.3 jit_solution(5909240886481675888)
XLA Ops:
  0.0 1.1 %home.1 = (bf16[8,6272]{1,0:T(8,128)(2,1)S(1)}, f32[8,128]{1,0:T(8,128)S(1)}) custom-call(s32[4]{0:T(128)} %r_0_.1, bf16[8,6144]{1,0:T(8,128)(2,1)} %r_1_.1, f32[1,6144]{1,0:T(1,128)} %bitcast.16, s32[2,8]{1,0:T(2,128)} %bitcast.17, f32[2,8]{1,0:T(2,128)} %bitcast.18), custom_call_target="tpu_custom_call" | custom-call | tf_op jit(solution)/shard_map/home/pallas_call | solution.py:208
  1.2 5.1 %collective-permute-start.1 = (bf16[8,6272]{1,0:T(8,128)(2,1)S(1)}, bf16[8,6272]{1,0:T(8,128)(2,1)S(1)}, u32[]{:S(2)}, u32[]{:S(2)}) collective-permute-start(bf16[8,6272]{1,0:T(8,128)(2,1)S(1)} %get-tuple-element.16.r_0_), channel_id=1, source_target_pairs={{0,6},{2,4},{4,2},{6,0},{1,7},{3,5},{5,3},{7,1},{8,14},{10,12},{12... | collective-permute-start | bytes 301064 | tf_op jit(solution)/shard_map/ppermute | solution.py:193
  6.4 3.7 %collective-permute-done.1.r_3_ = bf16[8,6272]{1,0:T(8,128)(2,1)S(1)} collective-permute-done((bf16[8,6272]{1,0:T(8,128)(2,1)S(1)}, bf16[8,6272]{1,0:T(8,128)(2,1)S(1)}, u32[]{:S(2)}, u32[]{:S(2)}) %collective-permute-start.1) | collective-permute-done | bytes 100384 | tf_op jit(solution)/shard_map/ppermute | solution.py:193
  10.1 1.0 %collective-permute-start.2 = (bf16[8,6272]{1,0:T(8,128)(2,1)S(1)}, bf16[8,6272]{1,0:T(8,128)(2,1)S(1)}, u32[]{:S(2)}, u32[]{:S(2)}) collective-permute-start(bf16[8,6272]{1,0:T(8,128)(2,1)S(1)} %collective-permute-done.1.r_3_), channel_id=1, source_target_pairs={{0,2},{2,0},{4,6},{6,4},{1,3},{3,1},{5,7},{7,5},{8,10},{10,8},{12,... | collective-permute-start | bytes 301064 | tf_op jit(solution)/shard_map/ppermute | solution.py:193
  11.1 0.7 %collective-permute-done.r_1_ = bf16[8,6272]{1,0:T(8,128)(2,1)S(1)} collective-permute-done((bf16[8,6272]{1,0:T(8,128)(2,1)S(1)}, bf16[8,6272]{1,0:T(8,128)(2,1)S(1)}, u32[]{:S(2)}, u32[]{:S(2)}) %collective-permute-start) | collective-permute-done | bytes 100384 | tf_op jit(solution)/shard_map/ppermute | solution.py:193
  11.8 2.9 %collective-permute-done.2.r_2_ = bf16[8,6272]{1,0:T(8,128)(2,1)S(1)} collective-permute-done((bf16[8,6272]{1,0:T(8,128)(2,1)S(1)}, bf16[8,6272]{1,0:T(8,128)(2,1)S(1)}, u32[]{:S(2)}, u32[]{:S(2)}) %collective-permute-start.2) | collective-permute-done | bytes 100384 | tf_op jit(solution)/shard_map/ppermute | solution.py:193
  14.7 0.5 pack_0.1
  15.2 1.7 %collective-permute-start.3 = (bf16[16,6144]{1,0:T(8,128)(2,1)S(1)}, bf16[16,6144]{1,0:T(8,128)(2,1)S(1)}, u32[]{:S(2)}, u32[]{:S(2)}) collective-permute-start(bf16[16,6144]{1,0:T(8,128)(2,1)S(1)} %get-tuple-element.18), channel_id=1, source_target_pairs={{0,8},{8,0},{16,24},{24,16},{1,9},{9,1},{17,25},{25,17},{2,10},{10... | collective-permute-start | bytes 589832 | tf_op jit(solution)/shard_map/ppermute | solution.py:193
  16.9 1.5 %collective-permute-start.4 = (bf16[16,6144]{1,0:T(8,128)(2,1)S(1)}, bf16[16,6144]{1,0:T(8,128)(2,1)S(1)}, u32[]{:S(2)}, u32[]{:S(2)}) collective-permute-start(bf16[16,6144]{1,0:T(8,128)(2,1)S(1)} %get-tuple-element.19), channel_id=1, source_target_pairs={{0,16},{8,24},{16,0},{24,8},{1,17},{9,25},{17,1},{25,9},{2,18},{10... | collective-permute-start | bytes 589832 | tf_op jit(solution)/shard_map/ppermute | solution.py:193
  18.5 0.3 collective-permute-start.5
  18.8 3.4 %collective-permute-done.3.r_1_ = bf16[16,6144]{1,0:T(8,128)(2,1)S(1)} collective-permute-done((bf16[16,6144]{1,0:T(8,128)(2,1)S(1)}, bf16[16,6144]{1,0:T(8,128)(2,1)S(1)}, u32[]{:S(2)}, u32[]{:S(2)}) %collective-permute-start.3) | collective-permute-done | bytes 196640 | tf_op jit(solution)/shard_map/ppermute | solution.py:193
  22.2 3.3 %collective-permute-done.4.r_2_ = bf16[16,6144]{1,0:T(8,128)(2,1)S(1)} collective-permute-done((bf16[16,6144]{1,0:T(8,128)(2,1)S(1)}, bf16[16,6144]{1,0:T(8,128)(2,1)S(1)}, u32[]{:S(2)}, u32[]{:S(2)}) %collective-permute-start.4) | collective-permute-done | bytes 196640 | tf_op jit(solution)/shard_map/ppermute | solution.py:193
  25.5 0.5 collective-permute-start.9
  26.0 0.9 %collective-permute-done.8.r_6_ = bf16[16,6144]{1,0:T(8,128)(2,1)S(1)} collective-permute-done((bf16[16,6144]{1,0:T(8,128)(2,1)S(1)}, bf16[16,6144]{1,0:T(8,128)(2,1)S(1)}, u32[]{:S(2)}, u32[]{:S(2)}) %collective-permute-start.8) | collective-permute-done | bytes 196640 | tf_op jit(solution)/shard_map/ppermute | solution.py:193
  27.0 0.3 collective-permute-done.9.r_7_
  27.3 4.0 %up_0.1.r_0_ = bf16[128,1024]{1,0:T(8,128)(2,1)S(1)} custom-call(bf16[16,6144]{1,0:T(8,128)(2,1)S(1)} %get-tuple-element.17.r_0_, bf16[16,6144]{1,0:T(8,128)(2,1)S(1)} %collective-permute-done.3.r_1_, bf16[16,6144]{1,0:T(8,128)(2,1)S(1)} %collective-permute-done.4.r_2_, bf16[16,6144]{1,0:T(8,128)(2,1)S(1)} %collective-permute-done.5.r_3_, ...), custom_call_target="tpu_custom_call" | custom-call | tf_op jit(solution)/shard_map/up_0/pallas_call | solution.py:250
  31.3 0.5 copy-done
  31.9 1.4 %down_0.1 = (f32[64,4608]{1,0:T(8,128)S(1)}, bf16[64,4608]{1,0:T(8,128)(2,1)S(1)}) custom-call(bf16[128,1024]{1,0:T(8,128)(2,1)S(1)} %up_0.1.r_0_, bf16[1024,6144]{1,0:T(8,128)(2,1)S(1)} %bitcast.7), custom_call_target="tpu_custom_call" | custom-call | flops 1207959552 | tf_op jit(solution)/shard_map/down_0/pallas_call | solution.py:265
  33.3 0.3 collective-permute-start.10
  33.6 0.6 down_1.1
  34.2 0.3 collective-permute-start.11
  34.5 1.2 %collective-permute-done.11.refs_3_ = bf16[64,1536]{1,0:T(8,128)(2,1)S(1)} collective-permute-done((bf16[64,1536]{1,0:T(8,128)(2,1)S(1)}, bf16[64,1536]{1,0:T(8,128)(2,1)S(1)}, u32[]{:S(2)}, u32[]{:S(2)}) %collective-permute-start.11) | collective-permute-done | bytes 196640 | tf_op jit(solution)/shard_map/ppermute | solution.py:193
  35.9 27.2 %all_to_all.5 = bf16[16,4,6144]{2,1,0:T(4,128)(2,1)S(1)} all-to-all(bf16[16,4,6144]{2,1,0:T(4,128)(2,1)S(1)} %join.1), channel_id=1, replica_groups=mesh['expert'=4,'chip'=4,'core'=2] {'expert','chip'}, dimensions={0} | all-to-all | bytes 1572864 | tf_op jit(solution)/shard_map/all_to_all | solution.py:283
  63.1 1.3 %mix.1 = bf16[8,6144]{1,0:T(8,128)(2,1)} custom-call(f32[8,128]{1,0:T(8,128)S(1)} %get-tuple-element.15.meta_ref, bf16[4,4,4,6144]{3,2,1,0:T(4,128)(2,1)S(1)} %bitcast.15), custom_call_target="tpu_custom_call" | custom-call | tf_op jit(solution)/shard_map/mix/pallas_call | solution.py:284
  (24 shorter events, 0.2 us)
Async XLA Ops:
  1.1 26.1 %slice-start = ((s8[12582912]{0:T(1024)(128)(4,1)}), s8[4194304]{0:T(1024)(128)(4,1)S(1)}, s32[]{:S(2)}) async-start(s8[12582912]{0:T(1024)(128)(4,1)} %bitcast.9), calls=%async_computation.1 | async-start | bytes 8388608
  1.2 26.1 %slice-start.3 = ((s8[12582912]{0:T(1024)(128)(4,1)}), s8[4194304]{0:T(1024)(128)(4,1)S(1)}, s32[]{:S(2)}) async-start(s8[12582912]{0:T(1024)(128)(4,1)} %bitcast.12), calls=%async_computation.4 | async-start | bytes 8388608
  1.2 26.1 %slice-start.1 = ((s8[12582912]{0:T(1024)(128)(4,1)}), s8[4194304]{0:T(1024)(128)(4,1)S(1)}, s32[]{:S(2)}) async-start(s8[12582912]{0:T(1024)(128)(4,1)} %bitcast.9), calls=%async_computation.2 | async-start | bytes 8388608
  1.2 26.1 %slice-start.2 = ((s8[12582912]{0:T(1024)(128)(4,1)}), s8[4194304]{0:T(1024)(128)(4,1)S(1)}, s32[]{:S(2)}) async-start(s8[12582912]{0:T(1024)(128)(4,1)} %bitcast.9), calls=%async_computation.3 | async-start | bytes 8388608
  1.2 26.1 %slice-start.4 = ((s8[12582912]{0:T(1024)(128)(4,1)}), s8[4194304]{0:T(1024)(128)(4,1)S(1)}, s32[]{:S(2)}) async-start(s8[12582912]{0:T(1024)(128)(4,1)} %bitcast.12), calls=%async_computation.5 | async-start | bytes 8388608
  1.2 26.1 %slice-start.5 = ((s8[12582912]{0:T(1024)(128)(4,1)}), s8[4194304]{0:T(1024)(128)(4,1)S(1)}, s32[]{:S(2)}) async-start(s8[12582912]{0:T(1024)(128)(4,1)} %bitcast.12), calls=%async_computation.6 | async-start | bytes 8388608
  1.2 8.9 %collective-permute-start.1 = (bf16[8,6272]{1,0:T(8,128)(2,1)S(1)}, bf16[8,6272]{1,0:T(8,128)(2,1)S(1)}, u32[]{:S(2)}, u32[]{:S(2)}) collective-permute-start(bf16[8,6272]{1,0:T(8,128)(2,1)S(1)} %get-tuple-element.16.r_0_), channel_id=1, source_target_pairs={{0,6},{2,4},{4,2},{6,0},{1,7},{3,5},{5,3},{7,1},{8,14},{10,12},{12... | collective-permute-start | bytes 301064 | tf_op jit(solution)/shard_map/ppermute | solution.py:193
  6.3 5.5 %collective-permute-start = (bf16[8,6272]{1,0:T(8,128)(2,1)S(1)}, bf16[8,6272]{1,0:T(8,128)(2,1)S(1)}, u32[]{:S(2)}, u32[]{:S(2)}) collective-permute-start(bf16[8,6272]{1,0:T(8,128)(2,1)S(1)} %get-tuple-element.16.r_0_), channel_id=1, source_target_pairs={{0,2},{2,0},{4,6},{6,4},{1,3},{3,1},{5,7},{7,5},{8,10},{10,8},{12,... | collective-permute-start | bytes 301064 | tf_op jit(solution)/shard_map/ppermute | solution.py:193
  10.1 4.6 %collective-permute-start.2 = (bf16[8,6272]{1,0:T(8,128)(2,1)S(1)}, bf16[8,6272]{1,0:T(8,128)(2,1)S(1)}, u32[]{:S(2)}, u32[]{:S(2)}) collective-permute-start(bf16[8,6272]{1,0:T(8,128)(2,1)S(1)} %collective-permute-done.1.r_3_), channel_id=1, source_target_pairs={{0,2},{2,0},{4,6},{6,4},{1,3},{3,1},{5,7},{7,5},{8,10},{10,8},{12,... | collective-permute-start | bytes 301064 | tf_op jit(solution)/shard_map/ppermute | solution.py:193
  15.2 7.0 %collective-permute-start.3 = (bf16[16,6144]{1,0:T(8,128)(2,1)S(1)}, bf16[16,6144]{1,0:T(8,128)(2,1)S(1)}, u32[]{:S(2)}, u32[]{:S(2)}) collective-permute-start(bf16[16,6144]{1,0:T(8,128)(2,1)S(1)} %get-tuple-element.18), channel_id=1, source_target_pairs={{0,8},{8,0},{16,24},{24,16},{1,9},{9,1},{17,25},{25,17},{2,10},{10... | collective-permute-start | bytes 589832 | tf_op jit(solution)/shard_map/ppermute | solution.py:193
  16.9 8.6 %collective-permute-start.4 = (bf16[16,6144]{1,0:T(8,128)(2,1)S(1)}, bf16[16,6144]{1,0:T(8,128)(2,1)S(1)}, u32[]{:S(2)}, u32[]{:S(2)}) collective-permute-start(bf16[16,6144]{1,0:T(8,128)(2,1)S(1)} %get-tuple-element.19), channel_id=1, source_target_pairs={{0,16},{8,24},{16,0},{24,8},{1,17},{9,25},{17,1},{25,9},{2,18},{10... | collective-permute-start | bytes 589832 | tf_op jit(solution)/shard_map/ppermute | solution.py:193
  18.5 7.1 %collective-permute-start.5 = (bf16[16,6144]{1,0:T(8,128)(2,1)S(1)}, bf16[16,6144]{1,0:T(8,128)(2,1)S(1)}, u32[]{:S(2)}, u32[]{:S(2)}) collective-permute-start(bf16[16,6144]{1,0:T(8,128)(2,1)S(1)} %get-tuple-element.20), channel_id=1, source_target_pairs={{0,24},{8,16},{16,8},{24,0},{1,25},{9,17},{17,9},{25,1},{2,26},{10... | collective-permute-start | bytes 589832 | tf_op jit(solution)/shard_map/ppermute | solution.py:193
  18.8 7.3 %collective-permute-start.6 = (bf16[16,6144]{1,0:T(8,128)(2,1)S(1)}, bf16[16,6144]{1,0:T(8,128)(2,1)S(1)}, u32[]{:S(2)}, u32[]{:S(2)}) collective-permute-start(bf16[16,6144]{1,0:T(8,128)(2,1)S(1)} %get-tuple-element.17.r_0_), channel_id=1, source_target_pairs={{0,1},{1,0},{2,3},{3,2},{4,5},{5,4},{6,7},{7,6},{8,9},{9,8},{10,11... | collective-permute-start | bytes 589832 | tf_op jit(solution)/shard_map/ppermute | solution.py:193
  22.2 3.8 %collective-permute-start.7 = (bf16[16,6144]{1,0:T(8,128)(2,1)S(1)}, bf16[16,6144]{1,0:T(8,128)(2,1)S(1)}, u32[]{:S(2)}, u32[]{:S(2)}) collective-permute-start(bf16[16,6144]{1,0:T(8,128)(2,1)S(1)} %collective-permute-done.3.r_1_), channel_id=1, source_target_pairs={{0,1},{1,0},{2,3},{3,2},{4,5},{5,4},{6,7},{7,6},{8,9},{9,8},{10,11... | collective-permute-start | bytes 589832 | tf_op jit(solution)/shard_map/ppermute | solution.py:193
  25.5 1.4 %collective-permute-start.8 = (bf16[16,6144]{1,0:T(8,128)(2,1)S(1)}, bf16[16,6144]{1,0:T(8,128)(2,1)S(1)}, u32[]{:S(2)}, u32[]{:S(2)}) collective-permute-start(bf16[16,6144]{1,0:T(8,128)(2,1)S(1)} %collective-permute-done.4.r_2_), channel_id=1, source_target_pairs={{0,1},{1,0},{2,3},{3,2},{4,5},{5,4},{6,7},{7,6},{8,9},{9,8},{10,11... | collective-permute-start | bytes 589832 | tf_op jit(solution)/shard_map/ppermute | solution.py:193
  25.5 1.7 %collective-permute-start.9 = (bf16[16,6144]{1,0:T(8,128)(2,1)S(1)}, bf16[16,6144]{1,0:T(8,128)(2,1)S(1)}, u32[]{:S(2)}, u32[]{:S(2)}) collective-permute-start(bf16[16,6144]{1,0:T(8,128)(2,1)S(1)} %collective-permute-done.5.r_3_), channel_id=1, source_target_pairs={{0,1},{1,0},{2,3},{3,2},{4,5},{5,4},{6,7},{7,6},{8,9},{9,8},{10,11... | collective-permute-start | bytes 589832 | tf_op jit(solution)/shard_map/ppermute | solution.py:193
  27.3 4.6 %copy-start = (bf16[1,1024,6144]{2,1,0:T(8,128)(2,1)S(1)}, bf16[1,1024,6144]{2,1,0:T(8,128)(2,1)}, u32[]{:S(2)}) copy-start(bf16[1,1024,6144]{2,1,0:T(8,128)(2,1)} %param.15) | copy-start | bytes 37748740
  33.3 2.4 %collective-permute-start.10 = (bf16[64,4608]{1,0:T(8,128)(2,1)S(1)}, bf16[64,4608]{1,0:T(8,128)(2,1)S(1)}, u32[]{:S(2)}, u32[]{:S(2)}) collective-permute-start(bf16[64,4608]{1,0:T(8,128)(2,1)S(1)} %get-tuple-element.22), channel_id=1, source_target_pairs={{0,1},{1,0},{2,3},{3,2},{4,5},{5,4},{6,7},{7,6},{8,9},{9,8},{10,11... | collective-permute-start | bytes 1769480 | tf_op jit(solution)/shard_map/ppermute | solution.py:193
  34.2 1.5 %collective-permute-start.11 = (bf16[64,1536]{1,0:T(8,128)(2,1)S(1)}, bf16[64,1536]{1,0:T(8,128)(2,1)S(1)}, u32[]{:S(2)}, u32[]{:S(2)}) collective-permute-start(bf16[64,1536]{1,0:T(8,128)(2,1)S(1)} %get-tuple-element.24), channel_id=1, source_target_pairs={{0,1},{1,0},{2,3},{3,2},{4,5},{5,4},{6,7},{7,6},{8,9},{9,8},{10,11... | collective-permute-start | bytes 589832 | tf_op jit(solution)/shard_map/ppermute | solution.py:193
where the time goes:
time: 64.5 us; the launch traced here: 64.3 us
  blocking collectives  27.2 us (42%)
  waiting for transfers between devices  16.5 us (26%)
  starting transfers between devices  10.8 us (17%)
  Pallas kernels  9.05 us (14%)
    all_to_all x1, blocking collectives, on_device(): lax.all_to_all(partial, ('expert', 'chip'), split_axis=0, concat_axis=0,...  27.2 us
    ppermute x12, waiting for transfers between devices, flip(): lax.ppermute(value, axis, [(i, i ^ mask) for i in range(lax.axis_size(axi...  16.5 us
    ppermute x12, starting transfers between devices, flip(): lax.ppermute(value, axis, [(i, i ^ mask) for i in range(lax.axis_size(axi...  10.8 us
    pallas_call x1, Pallas kernels, on_device(): pl.pallas_call(lambda *r, i=i: up_kernel(zs, depth, i, PARTS_IN, *r), out...  4.02 us
    pallas_call x2, Pallas kernels, on_device(): pl.pallas_call(lambda *r, start=start: down_kernel(start, *r), out_shape=...  1.99 us
  transfers between devices with their start and end apart: 12, of which 8 were waited for; matrix products, arithmetic and copies ran while one was open for 0% of the time, Pallas kernels for 1%

commit v1 on v0

--- a/solution.py
+++ b/solution.py
@@ -9,7 +9,6 @@
 MIB = 1 << 20
 LANES = 128
 MOST_VMEM = 67035136
-PARTS_IN = 1
 CUTS = (6,)
 TILE = 256
 MIX_PARTS = 6
@@ -26,8 +25,7 @@
 
 
 def home_kernel(depth, cap_hbm, tok_hbm, gain_hbm, routes_hbm, gates_hbm, *refs):
-    meta_ref, cap_ref, tok_ref, gain_ref, routes_ref, gates_ref, sem = refs[-7:]
-    exts = refs[:-7]
+    ext_ref, meta_ref, cap_ref, tok_ref, gain_ref, routes_ref, gates_ref, sem = refs
     small = [(cap_hbm, cap_ref), (routes_hbm, routes_ref), (gates_hbm, gates_ref)]
     pairs = small + [(tok_hbm, tok_ref), (gain_hbm, gain_ref)]
     copies = [pltpu.make_async_copy(src, dst, sem.at[i]) for i, (src, dst) in enumerate(pairs)]
@@ -56,22 +54,18 @@
     code = jnp.where(lane == 0, codes[0], jnp.where(lane == 1, codes[1], 0.0))
     gate = [upright(gates_ref[k:k + 1, :]) for k in range(2)]
     meta_ref[...] = code + jnp.where(lane == 2, gate[0], jnp.where(lane == 3, gate[1], 0.0))
-    step = width // len(exts)
-    exts[0][:, step:] = code.astype(jnp.bfloat16)
+    ext_ref[:, width:] = code.astype(jnp.bfloat16)
     for c in copies[3:]:
         c.wait()
     wide = tok_ref[...].astype(jnp.float32)
     scale = lax.rsqrt(jnp.mean(wide * wide, axis=-1, keepdims=True) + 1e-05)
-    normed = (wide * scale * gain_ref[...]).astype(jnp.bfloat16)
-    for i, ext_ref in enumerate(exts):
-        ext_ref[:, :step] = normed[:, i * step:(i + 1) * step]
-
-
-def pack_kernel(depth, zs, first, *refs):
-    sources = zs if first else 2 * zs
-    experts = len(refs) - sources
+    ext_ref[:, :width] = (wide * scale * gain_ref[...]).astype(jnp.bfloat16)
+
+
+def pack_kernel(depth, zs, *refs):
+    experts = len(refs) - zs
     me = lax.axis_index("expert")
-    ins, data, outs = refs[:zs], refs[sources - zs:sources], refs[sources:]
+    ins, outs = refs[:zs], refs[zs:]
     tok = ins[0].shape[0]
     width = outs[0].shape[1]
     rows = experts * zs * depth
@@ -87,42 +81,27 @@
         hit = (code[:, 0:1] == target) | (code[:, 1:2] == target)
         picks.append(jnp.where(hit & (o == i), 1.0, 0.0))
     pick = jnp.concatenate(picks, axis=0).T.astype(jnp.bfloat16)
-    normed = jnp.concatenate([r[:, :width].astype(jnp.float32) for r in data], axis=0).astype(jnp.bfloat16)
+    normed = jnp.concatenate([r[:, :width].astype(jnp.float32) for r in ins], axis=0).astype(jnp.bfloat16)
     packed = jnp.dot(pick, normed, preferred_element_type=jnp.float32).astype(jnp.bfloat16)
     step = zs * depth
     for i in range(experts):
         outs[i][...] = packed[i * step:(i + 1) * step]
 
 
-def up_kernel(zs, depth, part, parts, *refs):
-    experts = lax.axis_size("expert")
-    blocks, (gate_ref, up_ref), refs = refs[:CORES * experts], refs[CORES * experts:CORES * experts + 2], refs[CORES * experts + 2:]
-    before = ()
-    if part:
-        before, refs = refs[:2], refs[2:]
-    step, width = blocks[0].shape
-    outs = refs[:-1] if part < parts - 1 else refs[:-2]
-    x_ref = refs[len(outs)]
+def up_kernel(groups, depth, *refs):
+    gate_ref, up_ref, hid_ref, x_ref, h_ref = refs[-5:]
+    blocks = refs[:-5]
     rows = x_ref.shape[0]
-    for i, r in enumerate(blocks):
-        x_ref[i * step:(i + 1) * step, :] = r[...]
-    tile = 256
-    span = slice(part * width, (part + 1) * width)
-    for n in range(gate_ref.shape[1] // tile):
-        cols = slice(n * tile, (n + 1) * tile)
-        g = jnp.dot(x_ref[...], gate_ref[span, cols], preferred_element_type=jnp.float32)
-        u = jnp.dot(x_ref[...], up_ref[span, cols], preferred_element_type=jnp.float32)
-        if part:
-            g = g + before[0][:, cols]
-            u = u + before[1][:, cols]
-        if part < parts - 1:
-            outs[0][:, cols] = g
-            outs[1][:, cols] = u
-        else:
-            refs[-1][:, cols] = (g / (1.0 + jnp.exp(-g)) * u).astype(jnp.bfloat16)
-    if part < parts - 1:
-        return
-    hid_ref, h_ref = outs[0], refs[-1]
+    start = 0
+    for r in blocks:
+        x_ref[start:start + r.shape[0], :] = r[...]
+        start += r.shape[0]
+    for n in range(gate_ref.shape[1] // TILE):
+        cols = slice(n * TILE, (n + 1) * TILE)
+        g = jnp.dot(x_ref[...], gate_ref[:, cols], preferred_element_type=jnp.float32)
+        u = jnp.dot(x_ref[...], up_ref[:, cols], preferred_element_type=jnp.float32)
+        h_ref[:, cols] = (g / (1.0 + jnp.exp(-g)) * u).astype(jnp.bfloat16)
+    experts, zs = lax.axis_size("expert"), lax.axis_size("chip")
     chip, me = lax.axis_index("chip"), lax.axis_index("expert")
     row = lax.broadcasted_iota(jnp.int32, (rows, rows), 0)
     col = lax.broadcasted_iota(jnp.int32, (rows, rows), 1)
@@ -131,7 +110,14 @@
     block = jnp.zeros_like(e)
     for i in range(experts):
         block = jnp.where(e == (me ^ i), i, block)
-    source = ((side * experts + block) * zs + (z ^ chip)) * depth + slot
+    offset = z ^ chip
+    source, start = jnp.zeros_like(e), 0
+    for group in groups:
+        for i, o in enumerate(group):
+            place = start + (block * len(group) + i) * depth + slot
+            source = jnp.where(offset == o, place, source)
+        start += experts * len(group) * depth
+    source = source + side * (rows // CORES)
     order = jnp.where(source == col, 1.0, 0.0).astype(jnp.bfloat16)
     hid_ref[...] = jnp.dot(order, h_ref[...], preferred_element_type=jnp.float32).astype(jnp.bfloat16)
 
@@ -147,7 +133,7 @@
 
 def join_kernel(*refs):
     out_ref = refs[-1]
-    blocks, depth, width = out_ref.shape
+    blocks, depth, _ = out_ref.shape
     start = 0
     for kept_ref, sent_ref in zip(refs[:-1:2], refs[1:-1:2]):
         cols = slice(start, start + kept_ref.shape[1])
@@ -193,6 +179,11 @@
     return lax.ppermute(value, axis, [(i, i ^ mask) for i in range(lax.axis_size(axis))])
 
 
+def grouped(groups):
+    early = sum(groups[:-1], [])
+    return [early, groups[-1]]
+
+
 def on_device(tokens, norm_gain, routes, gate_weights, capacity, w_gate, w_up, w_down):
     experts, zs = lax.axis_size("expert"), lax.axis_size("chip")
     tok, width = tokens.shape
@@ -201,15 +192,12 @@
     swap = lambda v: flip(v, "core", 1)
     rows = CORES * experts * zs * depth
     f32, bf16 = jnp.float32, jnp.bfloat16
-    scope = jax.named_scope
-
-    part = width // PARTS_IN
-    sizes = [part + LANES] + [part] * (PARTS_IN - 1)
-    *exts, meta = pl.pallas_call(
+
+    ext, meta = pl.pallas_call(
         lambda *r: home_kernel(depth, *r),
-        out_shape=[VMEM((tok, n), bf16) for n in sizes] + [VMEM((tok, LANES), f32)],
+        out_shape=[VMEM((tok, width + LANES), bf16), VMEM((tok, LANES), f32)],
         in_specs=[whole(pl.ANY)] * 5,
-        out_specs=[whole()] * (PARTS_IN + 1),
+        out_specs=[whole()] * 2,
         scratch_shapes=[
             SMEM(capacity.shape, jnp.int32),
             VMEM((tok, width), bf16),
@@ -222,46 +210,47 @@
         name="home",
     )(capacity, tokens, norm_gain.reshape(1, width), routes.T, gate_weights.T)
 
-    gathered = []
-    for i in range(PARTS_IN):
-        near = {0: exts[i]}
-        for mask in flips(zs):
-            for o in list(near):
-                near[o ^ mask] = flip(near[o], "chip", mask)
-        gathered.append([near[o] for o in range(zs)])
-    acc = ()
-    for i in range(PARTS_IN):
-        first = i == 0
-        sources = gathered[0] + ([] if first else gathered[i])
+    near, groups = {0: ext}, [[0]]
+    masks = flips(zs)
+    for i, mask in enumerate(masks):
+        for o in list(near):
+            near[o ^ mask] = flip(near[o], "chip", mask)
+        if i >= len(masks) - 2:
+            known = sum(groups, [])
+            groups.append([o for o in near if o not in known])
+    groups = grouped(groups)
+    shared = [[], []]
+    for g, group in enumerate(groups):
         packed = pl.pallas_call(
-            lambda *r, first=first: pack_kernel(depth, zs, first, *r),
-            out_shape=[jax.ShapeDtypeStruct((zs * depth, part), bf16)] * experts,
-            in_specs=[whole()] * len(sources),
+            lambda *r, size=len(group): pack_kernel(depth, size, *r),
+            out_shape=[jax.ShapeDtypeStruct((len(group) * depth, width), bf16)] * experts,
+            in_specs=[whole()] * len(group),
             out_specs=[whole()] * experts,
             compiler_params=params(8),
-            cost_estimate=pl.CostEstimate(flops=10**11 if first else 10**6, bytes_accessed=0, transcendentals=0),
-            name=f"pack_{i}",
-        )(*sources)
-        arrived = [packed[0]] + [flip(packed[k], "expert", k) for k in range(1, experts)]
-        theirs = [swap(v) for v in arrived]
-        last = i == PARTS_IN - 1
-        total = jax.ShapeDtypeStruct((rows, hidden), f32)
-        scratch = [VMEM((rows, part), bf16)] + ([VMEM((rows, hidden), bf16)] if last else [])
-        acc = pl.pallas_call(
-            lambda *r, i=i: up_kernel(zs, depth, i, PARTS_IN, *r),
-            out_shape=[jax.ShapeDtypeStruct((rows, hidden), bf16)] if last else [total, total],
-            in_specs=[whole()] * (CORES * experts + 2 + len(acc)),
-            out_specs=[whole()] * (1 if last else 2),
-            scratch_shapes=scratch,
-            compiler_params=params(10 if rows <= 128 else 22),
-            name=f"up_{i}",
-        )(*arrived, *theirs, w_gate[0], w_up[0], *acc)
-    hid = acc[0]
+            cost_estimate=pl.CostEstimate(flops=10**11 if g == 0 else 10**6, bytes_accessed=0, transcendentals=0),
+        )(*[near[o] for o in group])
+        arrived = [packed[0]]
+        for k in range(1, experts):
+            arrived.append(flip(packed[k], "expert", k))
+        for k in range(experts):
+            shared[1].append(swap(arrived[k]))
+        shared[0] += arrived
+    blocks = shared[0] + shared[1]
+    hid = pl.pallas_call(
+        lambda *r: up_kernel(groups, depth, *r),
+        out_shape=jax.ShapeDtypeStruct((rows, hidden), bf16),
+        in_specs=[whole()] * (len(blocks) + 2),
+        out_specs=whole(),
+        scratch_shapes=[VMEM((rows, width), bf16), VMEM((rows, hidden), bf16)],
+        compiler_params=params(10 if rows <= 128 else 22),
+        name="up",
+    )(*blocks, w_gate[0], w_up[0])
+
     mine = rows // CORES
     tiles = width // TILE
     bounds = [0, *[tiles * k // 8 * TILE for k in CUTS], width]
     halves = []
-    for j, (start, stop) in enumerate(zip(bounds[:-1], bounds[1:])):
+    for start, stop in zip(bounds[:-1], bounds[1:]):
         kept, sent = pl.pallas_call(
             lambda *r, start=start: down_kernel(start, *r),
             out_shape=[jax.ShapeDtypeStruct((mine, stop - start), dtype) for dtype in (f32, bf16)],
@@ -269,7 +258,6 @@
             out_specs=[whole()] * 2,
             compiler_params=params(8),
             cost_estimate=pl.CostEstimate(flops=4 * mine * (stop - start) * hidden, bytes_accessed=0, transcendentals=0),
-            name=f"down_{j}",
         )(hid, w_down[0])
         halves += [kept, swap(sent)]
     partial = pl.pallas_call(
@@ -301,5 +289,4 @@
         everywhere, P(), everywhere, everywhere, P(),
         columns, columns, P("expert", ("chip", "core"), None),
     )
-    step = jax.shard_map(on_device, mesh=split, in_specs=in_specs, out_specs=everywhere, check_vma=False)
-    return step
+    return jax.shard_map(on_device, mesh=split, in_specs=in_specs, out_specs=everywhere, check_vma=False)

time: 64.5 us -> 65.9 us (1.022)
  starting transfers between devices: 10.8 us -> 13.7 us
  waiting for transfers between devices: 16.5 us -> 14.5 us
    ppermute x12 -> x19, starting transfers between devices: 10.8 us -> 13.7 us  [flip(): lax.ppermute(value, axis, [(i, i ^ mask) for i in range(lax.axis_size(axi...]
    ppermute x12 -> x19, waiting for transfers between devices: 16.5 us -> 14.5 us  [flip(): lax.ppermute(value, axis, [(i, i ^ mask) for i in range(lax.axis_size(axi...]
    pallas_call x3 -> x4, Pallas kernels: 5.63 us -> 5.9 us  [the longest x1 4.02 us: on_device(): pl.pallas_call(lambda *r: up_kernel(groups, depth, *r), out_shape=jax.Sha...]
  transfers between devices with their start and end apart: 12 -> 19, of which waited for: 8 -> 9; matrix products, arithmetic and copies ran while one was open for 0% -> 0% of each run, Pallas kernels for 1% -> 2%
where the time goes in v1:
time: 65.9 us; the launch traced here: 65.7 us
  blocking collectives  27.5 us (42%)
  waiting for transfers between devices  14.5 us (22%)
  starting transfers between devices  13.7 us (21%)
  Pallas kernels  9.32 us (14%)
    all_to_all x1, blocking collectives, on_device(): lax.all_to_all(partial, ('expert', 'chip'), split_axis=0, concat_axis=0,...  27.5 us
    ppermute x19, waiting for transfers between devices, flip(): lax.ppermute(value, axis, [(i, i ^ mask) for i in range(lax.axis_size(axi...  14.5 us
    ppermute x19, starting transfers between devices, flip(): lax.ppermute(value, axis, [(i, i ^ mask) for i in range(lax.axis_size(axi...  13.7 us
    pallas_call x1, Pallas kernels, on_device(): pl.pallas_call(lambda *r: up_kernel(groups, depth, *r), out_shape=jax.Sha...  4.02 us
    pallas_call x2, Pallas kernels, on_device(): pl.pallas_call(lambda *r, start=start: down_kernel(start, *r), out_shape=...  1.99 us
  transfers between devices with their start and end apart: 19, of which 9 were waited for; matrix products, arithmetic and copies ran while one was open for 0% of the time, Pallas kernels for 2%

profile of v1, /device:TPU:0, one launch (start us, length us, event | category | flops | bytes accessed | tf_op | source)
XLA Modules:
  0.0 65.7 jit_solution(4645855318108925846)
XLA Ops:
  0.0 1.1 %home.1 = (bf16[8,6272]{1,0:T(8,128)(2,1)S(1)}, f32[8,128]{1,0:T(8,128)S(1)}) custom-call(s32[4]{0:T(128)} %r_0_.1, bf16[8,6144]{1,0:T(8,128)(2,1)} %r_1_.1, f32[1,6144]{1,0:T(1,128)} %bitcast.16, s32[2,8]{1,0:T(2,128)} %bitcast.17, f32[2,8]{1,0:T(2,128)} %bitcast.18), custom_call_target="tpu_custom_call" | custom-call | tf_op jit(solution)/shard_map/home/pallas_call | solution.py:196
  1.2 5.1 %collective-permute-start = (bf16[8,6272]{1,0:T(8,128)(2,1)S(1)}, bf16[8,6272]{1,0:T(8,128)(2,1)S(1)}, u32[]{:S(2)}, u32[]{:S(2)}) collective-permute-start(bf16[8,6272]{1,0:T(8,128)(2,1)S(1)} %get-tuple-element.20.r_0_), channel_id=1, source_target_pairs={{0,6},{2,4},{4,2},{6,0},{1,7},{3,5},{5,3},{7,1},{8,14},{10,12},{12... | collective-permute-start | bytes 301064 | tf_op jit(solution)/shard_map/ppermute | solution.py:179
  6.4 3.7 %collective-permute-done.r_1_ = bf16[8,6272]{1,0:T(8,128)(2,1)S(1)} collective-permute-done((bf16[8,6272]{1,0:T(8,128)(2,1)S(1)}, bf16[8,6272]{1,0:T(8,128)(2,1)S(1)}, u32[]{:S(2)}, u32[]{:S(2)}) %collective-permute-start) | collective-permute-done | bytes 100384 | tf_op jit(solution)/shard_map/ppermute | solution.py:179
  10.1 1.0 %collective-permute-start.5 = (bf16[8,6272]{1,0:T(8,128)(2,1)S(1)}, bf16[8,6272]{1,0:T(8,128)(2,1)S(1)}, u32[]{:S(2)}, u32[]{:S(2)}) collective-permute-start(bf16[8,6272]{1,0:T(8,128)(2,1)S(1)} %collective-permute-done.r_1_), channel_id=1, source_target_pairs={{0,2},{2,0},{4,6},{6,4},{1,3},{3,1},{5,7},{7,5},{8,10},{10,8},{12,... | collective-permute-start | bytes 301064 | tf_op jit(solution)/shard_map/ppermute | solution.py:179
  11.4 1.5 %collective-permute-start.1 = (bf16[8,6144]{1,0:T(8,128)(2,1)S(1)}, bf16[8,6144]{1,0:T(8,128)(2,1)S(1)}, u32[]{:S(2)}, u32[]{:S(2)}) collective-permute-start(bf16[8,6144]{1,0:T(8,128)(2,1)S(1)} %get-tuple-element.22), channel_id=1, source_target_pairs={{0,8},{8,0},{16,24},{24,16},{1,9},{9,1},{17,25},{25,17},{2,10},{10... | collective-permute-start | bytes 294920 | tf_op jit(solution)/shard_map/ppermute | solution.py:179
  13.0 1.5 %collective-permute-start.2 = (bf16[8,6144]{1,0:T(8,128)(2,1)S(1)}, bf16[8,6144]{1,0:T(8,128)(2,1)S(1)}, u32[]{:S(2)}, u32[]{:S(2)}) collective-permute-start(bf16[8,6144]{1,0:T(8,128)(2,1)S(1)} %get-tuple-element.23), channel_id=1, source_target_pairs={{0,16},{8,24},{16,0},{24,8},{1,17},{9,25},{17,1},{25,9},{2,18},{10... | collective-permute-start | bytes 294920 | tf_op jit(solution)/shard_map/ppermute | solution.py:179
  14.5 0.5 collective-permute-start.3
  15.0 1.8 %collective-permute-done.1.r_1_ = bf16[8,6144]{1,0:T(8,128)(2,1)S(1)} collective-permute-done((bf16[8,6144]{1,0:T(8,128)(2,1)S(1)}, bf16[8,6144]{1,0:T(8,128)(2,1)S(1)}, u32[]{:S(2)}, u32[]{:S(2)}) %collective-permute-start.1) | collective-permute-done | bytes 98336 | tf_op jit(solution)/shard_map/ppermute | solution.py:179
  16.8 1.2 %collective-permute-done.2.r_2_ = bf16[8,6144]{1,0:T(8,128)(2,1)S(1)} collective-permute-done((bf16[8,6144]{1,0:T(8,128)(2,1)S(1)}, bf16[8,6144]{1,0:T(8,128)(2,1)S(1)}, u32[]{:S(2)}, u32[]{:S(2)}) %collective-permute-start.2) | collective-permute-done | bytes 98336 | tf_op jit(solution)/shard_map/ppermute | solution.py:179
  18.7 1.3 %collective-permute-done.3.r_3_ = bf16[8,6144]{1,0:T(8,128)(2,1)S(1)} collective-permute-done((bf16[8,6144]{1,0:T(8,128)(2,1)S(1)}, bf16[8,6144]{1,0:T(8,128)(2,1)S(1)}, u32[]{:S(2)}, u32[]{:S(2)}) %collective-permute-start.3) | collective-permute-done | bytes 98336 | tf_op jit(solution)/shard_map/ppermute | solution.py:179
  20.0 0.5 collective-permute-start.7
  20.5 1.5 %collective-permute-start.8 = (bf16[8,6144]{1,0:T(8,128)(2,1)S(1)}, bf16[8,6144]{1,0:T(8,128)(2,1)S(1)}, u32[]{:S(2)}, u32[]{:S(2)}) collective-permute-start(bf16[8,6144]{1,0:T(8,128)(2,1)S(1)} %get-tuple-element.28), channel_id=1, source_target_pairs={{0,24},{8,16},{16,8},{24,0},{1,25},{9,17},{17,9},{25,1},{2,26},{10... | collective-permute-start | bytes 294920 | tf_op jit(solution)/shard_map/ppermute | solution.py:179
  22.0 0.5 collective-permute-start.13
  22.5 1.5 %collective-permute-done.6.r_5_ = bf16[8,6144]{1,0:T(8,128)(2,1)S(1)} collective-permute-done((bf16[8,6144]{1,0:T(8,128)(2,1)S(1)}, bf16[8,6144]{1,0:T(8,128)(2,1)S(1)}, u32[]{:S(2)}, u32[]{:S(2)}) %collective-permute-start.6) | collective-permute-done | bytes 98336 | tf_op jit(solution)/shard_map/ppermute | solution.py:179
  24.1 2.7 %collective-permute-done.7.r_6_ = bf16[8,6144]{1,0:T(8,128)(2,1)S(1)} collective-permute-done((bf16[8,6144]{1,0:T(8,128)(2,1)S(1)}, bf16[8,6144]{1,0:T(8,128)(2,1)S(1)}, u32[]{:S(2)}, u32[]{:S(2)}) %collective-permute-start.7) | collective-permute-done | bytes 98336 | tf_op jit(solution)/shard_map/ppermute | solution.py:179
  26.7 0.5 collective-permute-start.16
  27.3 0.8 %collective-permute-done.15.r_14_ = bf16[8,6144]{1,0:T(8,128)(2,1)S(1)} collective-permute-done((bf16[8,6144]{1,0:T(8,128)(2,1)S(1)}, bf16[8,6144]{1,0:T(8,128)(2,1)S(1)}, u32[]{:S(2)}, u32[]{:S(2)}) %collective-permute-start.15) | collective-permute-done | bytes 98336 | tf_op jit(solution)/shard_map/ppermute | solution.py:179
  28.3 4.0 %up.1.r_0_ = bf16[128,1024]{1,0:T(8,128)(2,1)S(1)} custom-call(bf16[8,6144]{1,0:T(8,128)(2,1)S(1)} %get-tuple-element.21.r_0_, bf16[8,6144]{1,0:T(8,128)(2,1)S(1)} %collective-permute-done.1.r_1_, bf16[8,6144]{1,0:T(8,128)(2,1)S(1)} %collective-permute-done.2.r_2_, bf16[8,6144]{1,0:T(8,128)(2,1)S(1)} %collective-permute-done.3.r_3_, ...), custom_call_target="tpu_custom_call" | custom-call | tf_op jit(solution)/shard_map/up/pallas_call | solution.py:239
  32.3 0.5 copy-done
  32.8 1.4 %shard_map.84 = (f32[64,4608]{1,0:T(8,128)S(1)}, bf16[64,4608]{1,0:T(8,128)(2,1)S(1)}) custom-call(bf16[128,1024]{1,0:T(8,128)(2,1)S(1)} %up.1.r_0_, bf16[1024,6144]{1,0:T(8,128)(2,1)S(1)} %bitcast.7), custom_call_target="tpu_custom_call" | custom-call | flops 1207959552 | tf_op jit(solution)/shard_map/pallas_call | solution.py:254
  34.7 0.6 shard_map.85
  35.5 1.3 %collective-permute-done.18.refs_3_ = bf16[64,1536]{1,0:T(8,128)(2,1)S(1)} collective-permute-done((bf16[64,1536]{1,0:T(8,128)(2,1)S(1)}, bf16[64,1536]{1,0:T(8,128)(2,1)S(1)}, u32[]{:S(2)}, u32[]{:S(2)}) %collective-permute-start.18) | collective-permute-done | bytes 196640 | tf_op jit(solution)/shard_map/ppermute | solution.py:179
  37.0 27.5 %all_to_all.5 = bf16[16,4,6144]{2,1,0:T(4,128)(2,1)S(1)} all-to-all(bf16[16,4,6144]{2,1,0:T(4,128)(2,1)S(1)} %join.1), channel_id=1, replica_groups=mesh['expert'=4,'chip'=4,'core'=2] {'expert','chip'}, dimensions={0} | all-to-all | bytes 1572864 | tf_op jit(solution)/shard_map/all_to_all | solution.py:271
  64.4 1.3 %mix.1 = bf16[8,6144]{1,0:T(8,128)(2,1)} custom-call(f32[8,128]{1,0:T(8,128)S(1)} %get-tuple-element.19.meta_ref, bf16[4,4,4,6144]{3,2,1,0:T(4,128)(2,1)S(1)} %bitcast.15), custom_call_target="tpu_custom_call" | custom-call | tf_op jit(solution)/shard_map/mix/pallas_call | solution.py:272
  (39 shorter events, 2.1 us)
Async XLA Ops:
  1.1 27.1 %slice-start = ((s8[12582912]{0:T(1024)(128)(4,1)}), s8[4194304]{0:T(1024)(128)(4,1)S(1)}, s32[]{:S(2)}) async-start(s8[12582912]{0:T(1024)(128)(4,1)} %bitcast.9), calls=%async_computation.1 | async-start | bytes 8388608
  1.2 27.1 %slice-start.3 = ((s8[12582912]{0:T(1024)(128)(4,1)}), s8[4194304]{0:T(1024)(128)(4,1)S(1)}, s32[]{:S(2)}) async-start(s8[12582912]{0:T(1024)(128)(4,1)} %bitcast.12), calls=%async_computation.4 | async-start | bytes 8388608
  1.2 27.0 %slice-start.1 = ((s8[12582912]{0:T(1024)(128)(4,1)}), s8[4194304]{0:T(1024)(128)(4,1)S(1)}, s32[]{:S(2)}) async-start(s8[12582912]{0:T(1024)(128)(4,1)} %bitcast.9), calls=%async_computation.2 | async-start | bytes 8388608
  1.2 27.0 %slice-start.2 = ((s8[12582912]{0:T(1024)(128)(4,1)}), s8[4194304]{0:T(1024)(128)(4,1)S(1)}, s32[]{:S(2)}) async-start(s8[12582912]{0:T(1024)(128)(4,1)} %bitcast.9), calls=%async_computation.3 | async-start | bytes 8388608
  1.2 27.0 %slice-start.4 = ((s8[12582912]{0:T(1024)(128)(4,1)}), s8[4194304]{0:T(1024)(128)(4,1)S(1)}, s32[]{:S(2)}) async-start(s8[12582912]{0:T(1024)(128)(4,1)} %bitcast.12), calls=%async_computation.5 | async-start | bytes 8388608
  1.2 8.9 %collective-permute-start = (bf16[8,6272]{1,0:T(8,128)(2,1)S(1)}, bf16[8,6272]{1,0:T(8,128)(2,1)S(1)}, u32[]{:S(2)}, u32[]{:S(2)}) collective-permute-start(bf16[8,6272]{1,0:T(8,128)(2,1)S(1)} %get-tuple-element.20.r_0_), channel_id=1, source_target_pairs={{0,6},{2,4},{4,2},{6,0},{1,7},{3,5},{5,3},{7,1},{8,14},{10,12},{12... | collective-permute-start | bytes 301064 | tf_op jit(solution)/shard_map/ppermute | solution.py:179
  6.3 8.6 %collective-permute-start.4 = (bf16[8,6272]{1,0:T(8,128)(2,1)S(1)}, bf16[8,6272]{1,0:T(8,128)(2,1)S(1)}, u32[]{:S(2)}, u32[]{:S(2)}) collective-permute-start(bf16[8,6272]{1,0:T(8,128)(2,1)S(1)} %get-tuple-element.20.r_0_), channel_id=1, source_target_pairs={{0,2},{2,0},{4,6},{6,4},{1,3},{3,1},{5,7},{7,5},{8,10},{10,8},{12,... | collective-permute-start | bytes 301064 | tf_op jit(solution)/shard_map/ppermute | solution.py:179
  10.1 7.9 %collective-permute-start.5 = (bf16[8,6272]{1,0:T(8,128)(2,1)S(1)}, bf16[8,6272]{1,0:T(8,128)(2,1)S(1)}, u32[]{:S(2)}, u32[]{:S(2)}) collective-permute-start(bf16[8,6272]{1,0:T(8,128)(2,1)S(1)} %collective-permute-done.r_1_), channel_id=1, source_target_pairs={{0,2},{2,0},{4,6},{6,4},{1,3},{3,1},{5,7},{7,5},{8,10},{10,8},{12,... | collective-permute-start | bytes 301064 | tf_op jit(solution)/shard_map/ppermute | solution.py:179
  11.4 5.3 %collective-permute-start.1 = (bf16[8,6144]{1,0:T(8,128)(2,1)S(1)}, bf16[8,6144]{1,0:T(8,128)(2,1)S(1)}, u32[]{:S(2)}, u32[]{:S(2)}) collective-permute-start(bf16[8,6144]{1,0:T(8,128)(2,1)S(1)} %get-tuple-element.22), channel_id=1, source_target_pairs={{0,8},{8,0},{16,24},{24,16},{1,9},{9,1},{17,25},{25,17},{2,10},{10... | collective-permute-start | bytes 294920 | tf_op jit(solution)/shard_map/ppermute | solution.py:179
  13.0 5.0 %collective-permute-start.2 = (bf16[8,6144]{1,0:T(8,128)(2,1)S(1)}, bf16[8,6144]{1,0:T(8,128)(2,1)S(1)}, u32[]{:S(2)}, u32[]{:S(2)}) collective-permute-start(bf16[8,6144]{1,0:T(8,128)(2,1)S(1)} %get-tuple-element.23), channel_id=1, source_target_pairs={{0,16},{8,24},{16,0},{24,8},{1,17},{9,25},{17,1},{25,9},{2,18},{10... | collective-permute-start | bytes 294920 | tf_op jit(solution)/shard_map/ppermute | solution.py:179
  14.5 5.5 %collective-permute-start.3 = (bf16[8,6144]{1,0:T(8,128)(2,1)S(1)}, bf16[8,6144]{1,0:T(8,128)(2,1)S(1)}, u32[]{:S(2)}, u32[]{:S(2)}) collective-permute-start(bf16[8,6144]{1,0:T(8,128)(2,1)S(1)} %get-tuple-element.24), channel_id=1, source_target_pairs={{0,24},{8,16},{16,8},{24,0},{1,25},{9,17},{17,9},{25,1},{2,26},{10... | collective-permute-start | bytes 294920 | tf_op jit(solution)/shard_map/ppermute | solution.py:179
  15.0 5.5 %collective-permute-start.9 = (bf16[8,6144]{1,0:T(8,128)(2,1)S(1)}, bf16[8,6144]{1,0:T(8,128)(2,1)S(1)}, u32[]{:S(2)}, u32[]{:S(2)}) collective-permute-start(bf16[8,6144]{1,0:T(8,128)(2,1)S(1)} %get-tuple-element.21.r_0_), channel_id=1, source_target_pairs={{0,1},{1,0},{2,3},{3,2},{4,5},{5,4},{6,7},{7,6},{8,9},{9,8},{10,11... | collective-permute-start | bytes 294920 | tf_op jit(solution)/shard_map/ppermute | solution.py:179
  16.7 5.3 %collective-permute-start.10 = (bf16[8,6144]{1,0:T(8,128)(2,1)S(1)}, bf16[8,6144]{1,0:T(8,128)(2,1)S(1)}, u32[]{:S(2)}, u32[]{:S(2)}) collective-permute-start(bf16[8,6144]{1,0:T(8,128)(2,1)S(1)} %collective-permute-done.1.r_1_), channel_id=1, source_target_pairs={{0,1},{1,0},{2,3},{3,2},{4,5},{5,4},{6,7},{7,6},{8,9},{9,8},{10,11... | collective-permute-start | bytes 294920 | tf_op jit(solution)/shard_map/ppermute | solution.py:179
  18.0 4.1 %collective-permute-start.11 = (bf16[8,6144]{1,0:T(8,128)(2,1)S(1)}, bf16[8,6144]{1,0:T(8,128)(2,1)S(1)}, u32[]{:S(2)}, u32[]{:S(2)}) collective-permute-start(bf16[8,6144]{1,0:T(8,128)(2,1)S(1)} %collective-permute-done.2.r_2_), channel_id=1, source_target_pairs={{0,1},{1,0},{2,3},{3,2},{4,5},{5,4},{6,7},{7,6},{8,9},{9,8},{10,11... | collective-permute-start | bytes 294920 | tf_op jit(solution)/shard_map/ppermute | solution.py:179
  18.4 5.7 %collective-permute-start.6 = (bf16[8,6144]{1,0:T(8,128)(2,1)S(1)}, bf16[8,6144]{1,0:T(8,128)(2,1)S(1)}, u32[]{:S(2)}, u32[]{:S(2)}) collective-permute-start(bf16[8,6144]{1,0:T(8,128)(2,1)S(1)} %get-tuple-element.26), channel_id=1, source_target_pairs={{0,8},{8,0},{16,24},{24,16},{1,9},{9,1},{17,25},{25,17},{2,10},{10... | collective-permute-start | bytes 294920 | tf_op jit(solution)/shard_map/ppermute | solution.py:179
  20.0 6.7 %collective-permute-start.7 = (bf16[8,6144]{1,0:T(8,128)(2,1)S(1)}, bf16[8,6144]{1,0:T(8,128)(2,1)S(1)}, u32[]{:S(2)}, u32[]{:S(2)}) collective-permute-start(bf16[8,6144]{1,0:T(8,128)(2,1)S(1)} %get-tuple-element.27), channel_id=1, source_target_pairs={{0,16},{8,24},{16,0},{24,8},{1,17},{9,25},{17,1},{25,9},{2,18},{10... | collective-permute-start | bytes 294920 | tf_op jit(solution)/shard_map/ppermute | solution.py:179
  20.5 6.2 %collective-permute-start.8 = (bf16[8,6144]{1,0:T(8,128)(2,1)S(1)}, bf16[8,6144]{1,0:T(8,128)(2,1)S(1)}, u32[]{:S(2)}, u32[]{:S(2)}) collective-permute-start(bf16[8,6144]{1,0:T(8,128)(2,1)S(1)} %get-tuple-element.28), channel_id=1, source_target_pairs={{0,24},{8,16},{16,8},{24,0},{1,25},{9,17},{17,9},{25,1},{2,26},{10... | collective-permute-start | bytes 294920 | tf_op jit(solution)/shard_map/ppermute | solution.py:179
  22.0 5.2 %collective-permute-start.12 = (bf16[8,6144]{1,0:T(8,128)(2,1)S(1)}, bf16[8,6144]{1,0:T(8,128)(2,1)S(1)}, u32[]{:S(2)}, u32[]{:S(2)}) collective-permute-start(bf16[8,6144]{1,0:T(8,128)(2,1)S(1)} %collective-permute-done.3.r_3_), channel_id=1, source_target_pairs={{0,1},{1,0},{2,3},{3,2},{4,5},{5,4},{6,7},{7,6},{8,9},{9,8},{10,11... | collective-permute-start | bytes 294920 | tf_op jit(solution)/shard_map/ppermute | solution.py:179
  22.0 5.2 %collective-permute-start.13 = (bf16[8,6144]{1,0:T(8,128)(2,1)S(1)}, bf16[8,6144]{1,0:T(8,128)(2,1)S(1)}, u32[]{:S(2)}, u32[]{:S(2)}) collective-permute-start(bf16[8,6144]{1,0:T(8,128)(2,1)S(1)} %get-tuple-element.25.r_4_), channel_id=1, source_target_pairs={{0,1},{1,0},{2,3},{3,2},{4,5},{5,4},{6,7},{7,6},{8,9},{9,8},{10,11... | collective-permute-start | bytes 294920 | tf_op jit(solution)/shard_map/ppermute | solution.py:179
  24.1 3.2 %collective-permute-start.14 = (bf16[8,6144]{1,0:T(8,128)(2,1)S(1)}, bf16[8,6144]{1,0:T(8,128)(2,1)S(1)}, u32[]{:S(2)}, u32[]{:S(2)}) collective-permute-start(bf16[8,6144]{1,0:T(8,128)(2,1)S(1)} %collective-permute-done.6.r_5_), channel_id=1, source_target_pairs={{0,1},{1,0},{2,3},{3,2},{4,5},{5,4},{6,7},{7,6},{8,9},{9,8},{10,11... | collective-permute-start | bytes 294920 | tf_op jit(solution)/shard_map/ppermute | solution.py:179
  26.7 1.3 %collective-permute-start.15 = (bf16[8,6144]{1,0:T(8,128)(2,1)S(1)}, bf16[8,6144]{1,0:T(8,128)(2,1)S(1)}, u32[]{:S(2)}, u32[]{:S(2)}) collective-permute-start(bf16[8,6144]{1,0:T(8,128)(2,1)S(1)} %collective-permute-done.7.r_6_), channel_id=1, source_target_pairs={{0,1},{1,0},{2,3},{3,2},{4,5},{5,4},{6,7},{7,6},{8,9},{9,8},{10,11... | collective-permute-start | bytes 294920 | tf_op jit(solution)/shard_map/ppermute | solution.py:179
  26.7 1.5 %collective-permute-start.16 = (bf16[8,6144]{1,0:T(8,128)(2,1)S(1)}, bf16[8,6144]{1,0:T(8,128)(2,1)S(1)}, u32[]{:S(2)}, u32[]{:S(2)}) collective-permute-start(bf16[8,6144]{1,0:T(8,128)(2,1)S(1)} %collective-permute-done.8.r_7_), channel_id=1, source_target_pairs={{0,1},{1,0},{2,3},{3,2},{4,5},{5,4},{6,7},{7,6},{8,9},{9,8},{10,11... | collective-permute-start | bytes 294920 | tf_op jit(solution)/shard_map/ppermute | solution.py:179
  34.2 2.5 %collective-permute-start.17 = (bf16[64,4608]{1,0:T(8,128)(2,1)S(1)}, bf16[64,4608]{1,0:T(8,128)(2,1)S(1)}, u32[]{:S(2)}, u32[]{:S(2)}) collective-permute-start(bf16[64,4608]{1,0:T(8,128)(2,1)S(1)} %get-tuple-element.30), channel_id=1, source_target_pairs={{0,1},{1,0},{2,3},{3,2},{4,5},{5,4},{6,7},{7,6},{8,9},{9,8},{10,11... | collective-permute-start | bytes 1769480 | tf_op jit(solution)/shard_map/ppermute | solution.py:179
  35.3 1.5 %collective-permute-start.18 = (bf16[64,1536]{1,0:T(8,128)(2,1)S(1)}, bf16[64,1536]{1,0:T(8,128)(2,1)S(1)}, u32[]{:S(2)}, u32[]{:S(2)}) collective-permute-start(bf16[64,1536]{1,0:T(8,128)(2,1)S(1)} %get-tuple-element.32), channel_id=1, source_target_pairs={{0,1},{1,0},{2,3},{3,2},{4,5},{5,4},{6,7},{7,6},{8,9},{9,8},{10,11... | collective-permute-start | bytes 589832 | tf_op jit(solution)/shard_map/ppermute | solution.py:179
  (2 other events, 31.6 us)

commit v2 on v1

--- a/solution.py
+++ b/solution.py
@@ -10,7 +10,7 @@
 LANES = 128
 MOST_VMEM = 67035136
 CUTS = (6,)
-TILE = 256
+TILE = 512
 MIX_PARTS = 6
 VMEM = pltpu.VMEM
 SMEM = pltpu.SMEM
@@ -89,8 +89,8 @@
 
 
 def up_kernel(groups, depth, *refs):
-    gate_ref, up_ref, hid_ref, x_ref, h_ref = refs[-5:]
-    blocks = refs[:-5]
+    gate_ref, up_ref, _, hid_ref, x_ref, h_ref = refs[-6:]
+    blocks = refs[:-6]
     rows = x_ref.shape[0]
     start = 0
     for r in blocks:
@@ -239,12 +239,12 @@
     hid = pl.pallas_call(
         lambda *r: up_kernel(groups, depth, *r),
         out_shape=jax.ShapeDtypeStruct((rows, hidden), bf16),
-        in_specs=[whole()] * (len(blocks) + 2),
+        in_specs=[whole()] * (len(blocks) + 2) + [whole(pl.ANY)],
         out_specs=whole(),
         scratch_shapes=[VMEM((rows, width), bf16), VMEM((rows, hidden), bf16)],
         compiler_params=params(10 if rows <= 128 else 22),
         name="up",
-    )(*blocks, w_gate[0], w_up[0])
+    )(*blocks, w_gate[0], w_up[0], w_down[0])
 
     mine = rows // CORES
     tiles = width // TILE

time: 65.9 us -> 65 us (0.986)
  no operation moved by 1% of the time
where the time goes in v2:
time: 65 us; the launch traced here: 64.8 us
  blocking collectives  27.5 us (42%)
  waiting for transfers between devices  14.5 us (22%)
  starting transfers between devices  13.7 us (21%)
  Pallas kernels  8.89 us (14%)
    all_to_all x1, blocking collectives, on_device(): lax.all_to_all(partial, ('expert', 'chip'), split_axis=0, concat_axis=0,...  27.5 us
    ppermute x19, waiting for transfers between devices, flip(): lax.ppermute(value, axis, [(i, i ^ mask) for i in range(lax.axis_size(axi...  14.5 us
    ppermute x19, starting transfers between devices, flip(): lax.ppermute(value, axis, [(i, i ^ mask) for i in range(lax.axis_size(axi...  13.7 us
    pallas_call x1, Pallas kernels, on_device(): pl.pallas_call(lambda *r: up_kernel(groups, depth, *r), out_shape=jax.Sha...  3.6 us
    pallas_call x2, Pallas kernels, on_device(): pl.pallas_call(lambda *r, start=start: down_kernel(start, *r), out_shape=...  1.99 us
  transfers between devices with their start and end apart: 19, of which 9 were waited for; matrix products, arithmetic and copies ran while one was open for 0% of the time, Pallas kernels for 2%

profile of v2, /device:TPU:0, one launch (start us, length us, event | category | flops | bytes accessed | tf_op | source)
XLA Modules:
  0.0 64.8 jit_solution(17198073224037216201)
XLA Ops:
  0.0 1.1 %home.1 = (bf16[8,6272]{1,0:T(8,128)(2,1)S(1)}, f32[8,128]{1,0:T(8,128)S(1)}) custom-call(s32[4]{0:T(128)} %r_0_.1, bf16[8,6144]{1,0:T(8,128)(2,1)} %r_1_.1, f32[1,6144]{1,0:T(1,128)} %bitcast.19, s32[2,8]{1,0:T(2,128)} %bitcast.20, f32[2,8]{1,0:T(2,128)} %bitcast.21), custom_call_target="tpu_custom_call" | custom-call | tf_op jit(solution)/shard_map/home/pallas_call | solution.py:196
  1.2 5.1 %collective-permute-start = (bf16[8,6272]{1,0:T(8,128)(2,1)S(1)}, bf16[8,6272]{1,0:T(8,128)(2,1)S(1)}, u32[]{:S(2)}, u32[]{:S(2)}) collective-permute-start(bf16[8,6272]{1,0:T(8,128)(2,1)S(1)} %get-tuple-element.20.r_0_), channel_id=1, source_target_pairs={{0,6},{2,4},{4,2},{6,0},{1,7},{3,5},{5,3},{7,1},{8,14},{10,12},{12... | collective-permute-start | bytes 301064 | tf_op jit(solution)/shard_map/ppermute | solution.py:179
  6.4 3.7 %collective-permute-done.r_1_ = bf16[8,6272]{1,0:T(8,128)(2,1)S(1)} collective-permute-done((bf16[8,6272]{1,0:T(8,128)(2,1)S(1)}, bf16[8,6272]{1,0:T(8,128)(2,1)S(1)}, u32[]{:S(2)}, u32[]{:S(2)}) %collective-permute-start) | collective-permute-done | bytes 100384 | tf_op jit(solution)/shard_map/ppermute | solution.py:179
  10.1 1.0 %collective-permute-start.5 = (bf16[8,6272]{1,0:T(8,128)(2,1)S(1)}, bf16[8,6272]{1,0:T(8,128)(2,1)S(1)}, u32[]{:S(2)}, u32[]{:S(2)}) collective-permute-start(bf16[8,6272]{1,0:T(8,128)(2,1)S(1)} %collective-permute-done.r_1_), channel_id=1, source_target_pairs={{0,2},{2,0},{4,6},{6,4},{1,3},{3,1},{5,7},{7,5},{8,10},{10,8},{12,... | collective-permute-start | bytes 301064 | tf_op jit(solution)/shard_map/ppermute | solution.py:179
  11.5 1.5 %collective-permute-start.1 = (bf16[8,6144]{1,0:T(8,128)(2,1)S(1)}, bf16[8,6144]{1,0:T(8,128)(2,1)S(1)}, u32[]{:S(2)}, u32[]{:S(2)}) collective-permute-start(bf16[8,6144]{1,0:T(8,128)(2,1)S(1)} %get-tuple-element.22), channel_id=1, source_target_pairs={{0,8},{8,0},{16,24},{24,16},{1,9},{9,1},{17,25},{25,17},{2,10},{10... | collective-permute-start | bytes 294920 | tf_op jit(solution)/shard_map/ppermute | solution.py:179
  13.0 1.5 %collective-permute-start.2 = (bf16[8,6144]{1,0:T(8,128)(2,1)S(1)}, bf16[8,6144]{1,0:T(8,128)(2,1)S(1)}, u32[]{:S(2)}, u32[]{:S(2)}) collective-permute-start(bf16[8,6144]{1,0:T(8,128)(2,1)S(1)} %get-tuple-element.23), channel_id=1, source_target_pairs={{0,16},{8,24},{16,0},{24,8},{1,17},{9,25},{17,1},{25,9},{2,18},{10... | collective-permute-start | bytes 294920 | tf_op jit(solution)/shard_map/ppermute | solution.py:179
  14.5 0.5 collective-permute-start.3
  15.0 1.8 %collective-permute-done.1.r_1_ = bf16[8,6144]{1,0:T(8,128)(2,1)S(1)} collective-permute-done((bf16[8,6144]{1,0:T(8,128)(2,1)S(1)}, bf16[8,6144]{1,0:T(8,128)(2,1)S(1)}, u32[]{:S(2)}, u32[]{:S(2)}) %collective-permute-start.1) | collective-permute-done | bytes 98336 | tf_op jit(solution)/shard_map/ppermute | solution.py:179
  16.8 1.2 %collective-permute-done.2.r_2_ = bf16[8,6144]{1,0:T(8,128)(2,1)S(1)} collective-permute-done((bf16[8,6144]{1,0:T(8,128)(2,1)S(1)}, bf16[8,6144]{1,0:T(8,128)(2,1)S(1)}, u32[]{:S(2)}, u32[]{:S(2)}) %collective-permute-start.2) | collective-permute-done | bytes 98336 | tf_op jit(solution)/shard_map/ppermute | solution.py:179
  18.7 1.3 %collective-permute-done.3.r_3_ = bf16[8,6144]{1,0:T(8,128)(2,1)S(1)} collective-permute-done((bf16[8,6144]{1,0:T(8,128)(2,1)S(1)}, bf16[8,6144]{1,0:T(8,128)(2,1)S(1)}, u32[]{:S(2)}, u32[]{:S(2)}) %collective-permute-start.3) | collective-permute-done | bytes 98336 | tf_op jit(solution)/shard_map/ppermute | solution.py:179
  20.1 0.5 collective-permute-start.7
  20.6 1.5 %collective-permute-start.8 = (bf16[8,6144]{1,0:T(8,128)(2,1)S(1)}, bf16[8,6144]{1,0:T(8,128)(2,1)S(1)}, u32[]{:S(2)}, u32[]{:S(2)}) collective-permute-start(bf16[8,6144]{1,0:T(8,128)(2,1)S(1)} %get-tuple-element.28), channel_id=1, source_target_pairs={{0,24},{8,16},{16,8},{24,0},{1,25},{9,17},{17,9},{25,1},{2,26},{10... | collective-permute-start | bytes 294920 | tf_op jit(solution)/shard_map/ppermute | solution.py:179
  22.1 0.5 collective-permute-start.13
  22.6 1.5 %collective-permute-done.6.r_5_ = bf16[8,6144]{1,0:T(8,128)(2,1)S(1)} collective-permute-done((bf16[8,6144]{1,0:T(8,128)(2,1)S(1)}, bf16[8,6144]{1,0:T(8,128)(2,1)S(1)}, u32[]{:S(2)}, u32[]{:S(2)}) %collective-permute-start.6) | collective-permute-done | bytes 98336 | tf_op jit(solution)/shard_map/ppermute | solution.py:179
  24.1 2.6 %collective-permute-done.7.r_6_ = bf16[8,6144]{1,0:T(8,128)(2,1)S(1)} collective-permute-done((bf16[8,6144]{1,0:T(8,128)(2,1)S(1)}, bf16[8,6144]{1,0:T(8,128)(2,1)S(1)}, u32[]{:S(2)}, u32[]{:S(2)}) %collective-permute-start.7) | collective-permute-done | bytes 98336 | tf_op jit(solution)/shard_map/ppermute | solution.py:179
  26.8 0.5 collective-permute-start.16
  27.3 0.8 %collective-permute-done.15.r_14_ = bf16[8,6144]{1,0:T(8,128)(2,1)S(1)} collective-permute-done((bf16[8,6144]{1,0:T(8,128)(2,1)S(1)}, bf16[8,6144]{1,0:T(8,128)(2,1)S(1)}, u32[]{:S(2)}, u32[]{:S(2)}) %collective-permute-start.15) | collective-permute-done | bytes 98336 | tf_op jit(solution)/shard_map/ppermute | solution.py:179
  28.3 3.6 %up.1.r_0_ = bf16[128,1024]{1,0:T(8,128)(2,1)S(1)} custom-call(bf16[8,6144]{1,0:T(8,128)(2,1)S(1)} %get-tuple-element.21.r_0_, bf16[8,6144]{1,0:T(8,128)(2,1)S(1)} %collective-permute-done.1.r_1_, bf16[8,6144]{1,0:T(8,128)(2,1)S(1)} %collective-permute-done.2.r_2_, bf16[8,6144]{1,0:T(8,128)(2,1)S(1)} %collective-permute-done.3.r_3_, ...), custom_call_target="tpu_custom_call" | custom-call | tf_op jit(solution)/shard_map/up/pallas_call | solution.py:239
  31.9 1.4 %shard_map.84 = (f32[64,4608]{1,0:T(8,128)S(1)}, bf16[64,4608]{1,0:T(8,128)(2,1)S(1)}) custom-call(bf16[128,1024]{1,0:T(8,128)(2,1)S(1)} %up.1.r_0_, bf16[1024,6144]{1,0:T(8,128)(2,1)S(1)} %bitcast.10), custom_call_target="tpu_custom_call" | custom-call | flops 1207959552 | tf_op jit(solution)/shard_map/pallas_call | solution.py:254
  33.3 0.4 collective-permute-start.17
  33.8 0.6 shard_map.85
  34.6 1.3 %collective-permute-done.18.refs_3_ = bf16[64,1536]{1,0:T(8,128)(2,1)S(1)} collective-permute-done((bf16[64,1536]{1,0:T(8,128)(2,1)S(1)}, bf16[64,1536]{1,0:T(8,128)(2,1)S(1)}, u32[]{:S(2)}, u32[]{:S(2)}) %collective-permute-start.18) | collective-permute-done | bytes 196640 | tf_op jit(solution)/shard_map/ppermute | solution.py:179
  36.1 27.5 %all_to_all.5 = bf16[16,4,6144]{2,1,0:T(4,128)(2,1)S(1)} all-to-all(bf16[16,4,6144]{2,1,0:T(4,128)(2,1)S(1)} %join.1), channel_id=1, replica_groups=mesh['expert'=4,'chip'=4,'core'=2] {'expert','chip'}, dimensions={0} | all-to-all | bytes 1572864 | tf_op jit(solution)/shard_map/all_to_all | solution.py:271
  63.5 1.3 %mix.1 = bf16[8,6144]{1,0:T(8,128)(2,1)} custom-call(f32[8,128]{1,0:T(8,128)S(1)} %get-tuple-element.19.meta_ref, bf16[4,4,4,6144]{3,2,1,0:T(4,128)(2,1)S(1)} %bitcast.18), custom_call_target="tpu_custom_call" | custom-call | tf_op jit(solution)/shard_map/mix/pallas_call | solution.py:272
  (44 shorter events, 1.7 us)
Async XLA Ops:
  1.1 27.1 %slice-start = ((s8[12582912]{0:T(1024)(128)(4,1)}), s8[4194304]{0:T(1024)(128)(4,1)S(1)}, s32[]{:S(2)}) async-start(s8[12582912]{0:T(1024)(128)(4,1)} %bitcast.7), calls=%async_computation.1 | async-start | bytes 8388608
  1.2 27.1 %slice-start.3 = ((s8[12582912]{0:T(1024)(128)(4,1)}), s8[4194304]{0:T(1024)(128)(4,1)S(1)}, s32[]{:S(2)}) async-start(s8[12582912]{0:T(1024)(128)(4,1)} %bitcast.12), calls=%async_computation.4 | async-start | bytes 8388608
  1.2 27.1 %slice-start.6 = ((s8[12582912]{0:T(1024)(128)(4,1)}), s8[4194304]{0:T(1024)(128)(4,1)S(1)}, s32[]{:S(2)}) async-start(s8[12582912]{0:T(1024)(128)(4,1)} %bitcast.15), calls=%async_computation.7 | async-start | bytes 8388608
  1.2 27.1 %slice-start.1 = ((s8[12582912]{0:T(1024)(128)(4,1)}), s8[4194304]{0:T(1024)(128)(4,1)S(1)}, s32[]{:S(2)}) async-start(s8[12582912]{0:T(1024)(128)(4,1)} %bitcast.7), calls=%async_computation.2 | async-start | bytes 8388608
  1.2 27.1 %slice-start.2 = ((s8[12582912]{0:T(1024)(128)(4,1)}), s8[4194304]{0:T(1024)(128)(4,1)S(1)}, s32[]{:S(2)}) async-start(s8[12582912]{0:T(1024)(128)(4,1)} %bitcast.7), calls=%async_computation.3 | async-start | bytes 8388608
  1.2 8.9 %collective-permute-start = (bf16[8,6272]{1,0:T(8,128)(2,1)S(1)}, bf16[8,6272]{1,0:T(8,128)(2,1)S(1)}, u32[]{:S(2)}, u32[]{:S(2)}) collective-permute-start(bf16[8,6272]{1,0:T(8,128)(2,1)S(1)} %get-tuple-element.20.r_0_), channel_id=1, source_target_pairs={{0,6},{2,4},{4,2},{6,0},{1,7},{3,5},{5,3},{7,1},{8,14},{10,12},{12... | collective-permute-start | bytes 301064 | tf_op jit(solution)/shard_map/ppermute | solution.py:179
  6.4 8.6 %collective-permute-start.4 = (bf16[8,6272]{1,0:T(8,128)(2,1)S(1)}, bf16[8,6272]{1,0:T(8,128)(2,1)S(1)}, u32[]{:S(2)}, u32[]{:S(2)}) collective-permute-start(bf16[8,6272]{1,0:T(8,128)(2,1)S(1)} %get-tuple-element.20.r_0_), channel_id=1, source_target_pairs={{0,2},{2,0},{4,6},{6,4},{1,3},{3,1},{5,7},{7,5},{8,10},{10,8},{12,... | collective-permute-start | bytes 301064 | tf_op jit(solution)/shard_map/ppermute | solution.py:179
  10.1 7.9 %collective-permute-start.5 = (bf16[8,6272]{1,0:T(8,128)(2,1)S(1)}, bf16[8,6272]{1,0:T(8,128)(2,1)S(1)}, u32[]{:S(2)}, u32[]{:S(2)}) collective-permute-start(bf16[8,6272]{1,0:T(8,128)(2,1)S(1)} %collective-permute-done.r_1_), channel_id=1, source_target_pairs={{0,2},{2,0},{4,6},{6,4},{1,3},{3,1},{5,7},{7,5},{8,10},{10,8},{12,... | collective-permute-start | bytes 301064 | tf_op jit(solution)/shard_map/ppermute | solution.py:179
  11.5 5.3 %collective-permute-start.1 = (bf16[8,6144]{1,0:T(8,128)(2,1)S(1)}, bf16[8,6144]{1,0:T(8,128)(2,1)S(1)}, u32[]{:S(2)}, u32[]{:S(2)}) collective-permute-start(bf16[8,6144]{1,0:T(8,128)(2,1)S(1)} %get-tuple-element.22), channel_id=1, source_target_pairs={{0,8},{8,0},{16,24},{24,16},{1,9},{9,1},{17,25},{25,17},{2,10},{10... | collective-permute-start | bytes 294920 | tf_op jit(solution)/shard_map/ppermute | solution.py:179
  13.0 5.0 %collective-permute-start.2 = (bf16[8,6144]{1,0:T(8,128)(2,1)S(1)}, bf16[8,6144]{1,0:T(8,128)(2,1)S(1)}, u32[]{:S(2)}, u32[]{:S(2)}) collective-permute-start(bf16[8,6144]{1,0:T(8,128)(2,1)S(1)} %get-tuple-element.23), channel_id=1, source_target_pairs={{0,16},{8,24},{16,0},{24,8},{1,17},{9,25},{17,1},{25,9},{2,18},{10... | collective-permute-start | bytes 294920 | tf_op jit(solution)/shard_map/ppermute | solution.py:179
  14.5 5.5 %collective-permute-start.3 = (bf16[8,6144]{1,0:T(8,128)(2,1)S(1)}, bf16[8,6144]{1,0:T(8,128)(2,1)S(1)}, u32[]{:S(2)}, u32[]{:S(2)}) collective-permute-start(bf16[8,6144]{1,0:T(8,128)(2,1)S(1)} %get-tuple-element.24), channel_id=1, source_target_pairs={{0,24},{8,16},{16,8},{24,0},{1,25},{9,17},{17,9},{25,1},{2,26},{10... | collective-permute-start | bytes 294920 | tf_op jit(solution)/shard_map/ppermute | solution.py:179
  15.0 5.5 %collective-permute-start.9 = (bf16[8,6144]{1,0:T(8,128)(2,1)S(1)}, bf16[8,6144]{1,0:T(8,128)(2,1)S(1)}, u32[]{:S(2)}, u32[]{:S(2)}) collective-permute-start(bf16[8,6144]{1,0:T(8,128)(2,1)S(1)} %get-tuple-element.21.r_0_), channel_id=1, source_target_pairs={{0,1},{1,0},{2,3},{3,2},{4,5},{5,4},{6,7},{7,6},{8,9},{9,8},{10,11... | collective-permute-start | bytes 294920 | tf_op jit(solution)/shard_map/ppermute | solution.py:179
  16.8 5.3 %collective-permute-start.10 = (bf16[8,6144]{1,0:T(8,128)(2,1)S(1)}, bf16[8,6144]{1,0:T(8,128)(2,1)S(1)}, u32[]{:S(2)}, u32[]{:S(2)}) collective-permute-start(bf16[8,6144]{1,0:T(8,128)(2,1)S(1)} %collective-permute-done.1.r_1_), channel_id=1, source_target_pairs={{0,1},{1,0},{2,3},{3,2},{4,5},{5,4},{6,7},{7,6},{8,9},{9,8},{10,11... | collective-permute-start | bytes 294920 | tf_op jit(solution)/shard_map/ppermute | solution.py:179
  18.0 4.1 %collective-permute-start.11 = (bf16[8,6144]{1,0:T(8,128)(2,1)S(1)}, bf16[8,6144]{1,0:T(8,128)(2,1)S(1)}, u32[]{:S(2)}, u32[]{:S(2)}) collective-permute-start(bf16[8,6144]{1,0:T(8,128)(2,1)S(1)} %collective-permute-done.2.r_2_), channel_id=1, source_target_pairs={{0,1},{1,0},{2,3},{3,2},{4,5},{5,4},{6,7},{7,6},{8,9},{9,8},{10,11... | collective-permute-start | bytes 294920 | tf_op jit(solution)/shard_map/ppermute | solution.py:179
  18.4 5.7 %collective-permute-start.6 = (bf16[8,6144]{1,0:T(8,128)(2,1)S(1)}, bf16[8,6144]{1,0:T(8,128)(2,1)S(1)}, u32[]{:S(2)}, u32[]{:S(2)}) collective-permute-start(bf16[8,6144]{1,0:T(8,128)(2,1)S(1)} %get-tuple-element.26), channel_id=1, source_target_pairs={{0,8},{8,0},{16,24},{24,16},{1,9},{9,1},{17,25},{25,17},{2,10},{10... | collective-permute-start | bytes 294920 | tf_op jit(solution)/shard_map/ppermute | solution.py:179
  20.1 6.7 %collective-permute-start.7 = (bf16[8,6144]{1,0:T(8,128)(2,1)S(1)}, bf16[8,6144]{1,0:T(8,128)(2,1)S(1)}, u32[]{:S(2)}, u32[]{:S(2)}) collective-permute-start(bf16[8,6144]{1,0:T(8,128)(2,1)S(1)} %get-tuple-element.27), channel_id=1, source_target_pairs={{0,16},{8,24},{16,0},{24,8},{1,17},{9,25},{17,1},{25,9},{2,18},{10... | collective-permute-start | bytes 294920 | tf_op jit(solution)/shard_map/ppermute | solution.py:179
  20.6 6.2 %collective-permute-start.8 = (bf16[8,6144]{1,0:T(8,128)(2,1)S(1)}, bf16[8,6144]{1,0:T(8,128)(2,1)S(1)}, u32[]{:S(2)}, u32[]{:S(2)}) collective-permute-start(bf16[8,6144]{1,0:T(8,128)(2,1)S(1)} %get-tuple-element.28), channel_id=1, source_target_pairs={{0,24},{8,16},{16,8},{24,0},{1,25},{9,17},{17,9},{25,1},{2,26},{10... | collective-permute-start | bytes 294920 | tf_op jit(solution)/shard_map/ppermute | solution.py:179
  22.1 5.2 %collective-permute-start.12 = (bf16[8,6144]{1,0:T(8,128)(2,1)S(1)}, bf16[8,6144]{1,0:T(8,128)(2,1)S(1)}, u32[]{:S(2)}, u32[]{:S(2)}) collective-permute-start(bf16[8,6144]{1,0:T(8,128)(2,1)S(1)} %collective-permute-done.3.r_3_), channel_id=1, source_target_pairs={{0,1},{1,0},{2,3},{3,2},{4,5},{5,4},{6,7},{7,6},{8,9},{9,8},{10,11... | collective-permute-start | bytes 294920 | tf_op jit(solution)/shard_map/ppermute | solution.py:179
  22.1 5.2 %collective-permute-start.13 = (bf16[8,6144]{1,0:T(8,128)(2,1)S(1)}, bf16[8,6144]{1,0:T(8,128)(2,1)S(1)}, u32[]{:S(2)}, u32[]{:S(2)}) collective-permute-start(bf16[8,6144]{1,0:T(8,128)(2,1)S(1)} %get-tuple-element.25.r_4_), channel_id=1, source_target_pairs={{0,1},{1,0},{2,3},{3,2},{4,5},{5,4},{6,7},{7,6},{8,9},{9,8},{10,11... | collective-permute-start | bytes 294920 | tf_op jit(solution)/shard_map/ppermute | solution.py:179
  24.1 3.2 %collective-permute-start.14 = (bf16[8,6144]{1,0:T(8,128)(2,1)S(1)}, bf16[8,6144]{1,0:T(8,128)(2,1)S(1)}, u32[]{:S(2)}, u32[]{:S(2)}) collective-permute-start(bf16[8,6144]{1,0:T(8,128)(2,1)S(1)} %collective-permute-done.6.r_5_), channel_id=1, source_target_pairs={{0,1},{1,0},{2,3},{3,2},{4,5},{5,4},{6,7},{7,6},{8,9},{9,8},{10,11... | collective-permute-start | bytes 294920 | tf_op jit(solution)/shard_map/ppermute | solution.py:179
  26.8 1.3 %collective-permute-start.15 = (bf16[8,6144]{1,0:T(8,128)(2,1)S(1)}, bf16[8,6144]{1,0:T(8,128)(2,1)S(1)}, u32[]{:S(2)}, u32[]{:S(2)}) collective-permute-start(bf16[8,6144]{1,0:T(8,128)(2,1)S(1)} %collective-permute-done.7.r_6_), channel_id=1, source_target_pairs={{0,1},{1,0},{2,3},{3,2},{4,5},{5,4},{6,7},{7,6},{8,9},{9,8},{10,11... | collective-permute-start | bytes 294920 | tf_op jit(solution)/shard_map/ppermute | solution.py:179
  26.8 1.5 %collective-permute-start.16 = (bf16[8,6144]{1,0:T(8,128)(2,1)S(1)}, bf16[8,6144]{1,0:T(8,128)(2,1)S(1)}, u32[]{:S(2)}, u32[]{:S(2)}) collective-permute-start(bf16[8,6144]{1,0:T(8,128)(2,1)S(1)} %collective-permute-done.8.r_7_), channel_id=1, source_target_pairs={{0,1},{1,0},{2,3},{3,2},{4,5},{5,4},{6,7},{7,6},{8,9},{9,8},{10,11... | collective-permute-start | bytes 294920 | tf_op jit(solution)/shard_map/ppermute | solution.py:179
  33.3 2.5 %collective-permute-start.17 = (bf16[64,4608]{1,0:T(8,128)(2,1)S(1)}, bf16[64,4608]{1,0:T(8,128)(2,1)S(1)}, u32[]{:S(2)}, u32[]{:S(2)}) collective-permute-start(bf16[64,4608]{1,0:T(8,128)(2,1)S(1)} %get-tuple-element.30), channel_id=1, source_target_pairs={{0,1},{1,0},{2,3},{3,2},{4,5},{5,4},{6,7},{7,6},{8,9},{9,8},{10,11... | collective-permute-start | bytes 1769480 | tf_op jit(solution)/shard_map/ppermute | solution.py:179
  34.4 1.5 %collective-permute-start.18 = (bf16[64,1536]{1,0:T(8,128)(2,1)S(1)}, bf16[64,1536]{1,0:T(8,128)(2,1)S(1)}, u32[]{:S(2)}, u32[]{:S(2)}) collective-permute-start(bf16[64,1536]{1,0:T(8,128)(2,1)S(1)} %get-tuple-element.32), channel_id=1, source_target_pairs={{0,1},{1,0},{2,3},{3,2},{4,5},{5,4},{6,7},{7,6},{8,9},{9,8},{10,11... | collective-permute-start | bytes 589832 | tf_op jit(solution)/shard_map/ppermute | solution.py:179
  (4 other events, 108.2 us)
